TPU v7x, 256 devices: a 4x2x16 block of a 4x16x16 slice. The times are simulated.
256 devices in a mesh: clip: 2 (over y), ha: 64 (over x, z), ta: 2 (over core).
Axes of the slice: x: 4, y: 2, z: 16, core: 2. Of those that a mesh axis runs over, the one named last changes fastest.
The devices are a block of a 4x16x16 slice.
Arguments:
- latent_tokens: bfloat16 [16, 4096, 64], P('clip', ('ha', 'ta')), parts along dimension 0, may hold values from -8 to 8
- w_in: bfloat16 [3, 3, 3, 16, 384], replicated, may hold values from -0.3125 to 0.3125
- b_in: float32 [384], replicated, may hold values from -3 to 3
- gn_gain: float32 [384], replicated, may hold values from 0.1 to 1.9
- gn_shift: float32 [384], replicated, may hold values from -3 to 3
- w_mid: bfloat16 [3, 3, 3, 384, 384], replicated, may hold values from -0.109375 to 0.109375
- b_mid: float32 [384], replicated, may hold values from -3 to 3
Outputs:
- decoded: bfloat16 [16, 128, 128, 384], P(('clip', 'ta'), 'ha'), parts along dimension 0
There are 2 independent parts, one for each index of `clip`. A program takes and returns all parts, laid end to end along the dimension named above; an argument that names none is the same for every part. Nothing has to cross between parts.
All inputs are finite; a program needn't handle non-finite values.
Results may differ from a plain program's by a relative error of at most 0.0054.
Values may be sent and summed in bfloat16 or wider, within the bound.
A program may use at most 64 MiB of HBM per device.

v0:
```python
import functools

import jax
import jax.numpy as jnp
from jax import lax
from jax.sharding import Mesh
from jax.sharding import PartitionSpec as P

GROUPS = 32
H_DEV = 2
W = 128
HA = ("ha_0", "ha_1")
HA_TA = ("ha_0", "ha_1", "ta")


eps = 1e-06


def passed_along(value, axis, by):
    devices = lax.axis_size(axis)
    pairs = [(i, i + by) for i in range(devices) if 0 <= i + by < devices]
    return lax.ppermute(value, axis, pairs)


def extended_2(value, sides, width):
    for axis, dim in sides:
        devices, length = (lax.axis_size(axis), value.shape[dim])
        up = [(i, (i + 1) % devices) for i in range(devices - 1)]
        down = [(j, i) for i, j in up]
        last = lax.slice_in_dim(value, length - width, length, axis=dim)
        first = lax.slice_in_dim(value, 0, width, axis=dim)
        before = lax.ppermute(last, axis, up)
        after = lax.ppermute(first, axis, down)
        value = jnp.concatenate([before, value, after], axis=dim)
    return value


def by_axis(value, axes):
    return functools.reduce(lax.psum, axes, value)


def unpatch(tokens, rows, cols):
    frames = tokens.shape[0]
    latent_ch = tokens.shape[2] // 4
    blocks = tokens.reshape(frames, rows // 2, cols // 2, 2, 2, latent_ch)
    return blocks.transpose(0, 1, 3, 2, 4, 5).reshape(frames, rows, cols, latent_ch)


def pad_cols(field):
    return jnp.pad(field, ((0, 0), (0, 0), (1, 1), (0, 0)))


def input_conv(padded, w_in, b_in, frames, rows, cols):
    pieces = [
        padded[frame_tap : frame_tap + frames, row_tap : row_tap + rows, col_tap : col_tap + cols]
        for frame_tap in range(3)
        for row_tap in range(3)
        for col_tap in range(3)
    ]
    stacked = jnp.concatenate(pieces, axis=-1).reshape(frames * rows * cols, -1)
    result = jnp.dot(
        stacked, w_in.reshape(stacked.shape[1], -1), preferred_element_type=jnp.float32
    )
    return (result + b_in).reshape(frames, rows, cols, -1)


def middle_conv(padded, w_mid, frames, rows, cols):
    channels = padded.shape[-1]
    total = jnp.zeros((frames * rows * cols, w_mid.shape[-1]), jnp.float32)
    for frame_tap in range(3):
        for row_tap in range(3):
            slab = jnp.concatenate(
                [
                    padded[
                        frame_tap : frame_tap + frames,
                        row_tap : row_tap + rows,
                        col_tap : col_tap + cols,
                    ]
                    for col_tap in range(3)
                ],
                axis=-1,
            ).reshape(frames * rows * cols, 3 * channels)
            total = total + jnp.dot(
                slab,
                w_mid[frame_tap, row_tap].reshape(3 * channels, -1),
                preferred_element_type=jnp.float32,
            )
    return total.reshape(frames, rows, cols, -1)


def group_totals(field):
    grouped = field.reshape(-1, GROUPS, field.shape[-1] // GROUPS)
    return jnp.sum(grouped, axis=(0, 2))


def normalize(hidden, mean, var, gn_gain, gn_shift):
    members = hidden.shape[-1] // GROUPS
    mean_chan = jnp.repeat(mean, members)
    scale_chan = jnp.repeat(lax.rsqrt(var + eps), members)
    scaled = (hidden.astype(jnp.float32) - mean_chan) * scale_chan * gn_gain + gn_shift
    return jax.nn.silu(scaled).astype(jnp.bfloat16)


def body(latent_tokens, w_in, b_in, gn_gain, gn_shift, w_mid, b_mid):
    rows = H_DEV
    cols = W
    moved = lax.all_to_all(latent_tokens, "ta", split_axis=0, concat_axis=1, tiled=True)
    latent = unpatch(moved, rows, cols)
    frames = latent.shape[0]
    earlier = passed_along(latent, "ta", 1)
    extended = jnp.concatenate([earlier, latent], axis=0)
    framed = extended_2(extended, ((HA, 1),), 2)
    wide_hidden = input_conv(pad_cols(framed), w_in, b_in, frames + 2, rows + 2, cols).astype(
        jnp.bfloat16
    )
    hidden = wide_hidden[2:, 1 : rows + 1]
    values = lax.optimization_barrier(hidden).astype(jnp.float32)
    members = values.shape[-1] // GROUPS
    count = float(lax.axis_size(HA) * lax.axis_size("ta") * frames * rows * cols * members)
    sums, squares = (
        by_axis(group_totals(values), HA_TA),
        by_axis(group_totals(values * values), HA_TA),
    )
    mean = sums / count
    var = squares / count - mean * mean
    active = normalize(wide_hidden, mean, var, gn_gain, gn_shift)
    frame_pos = lax.axis_index("ta") * frames + jnp.arange(frames + 2, dtype=jnp.int32) - 2
    row_pos = lax.axis_index(HA) * rows + jnp.arange(rows + 2, dtype=jnp.int32) - 1
    inside = (
        (frame_pos >= 0)[:, None]
        & (row_pos >= 0)[None, :]
        & (row_pos < rows * lax.axis_size(HA))[None, :]
    )
    padded = jnp.where(inside[:, :, None, None], active, jnp.zeros_like(active))
    branch = middle_conv(pad_cols(padded), w_mid, frames, rows, cols)
    return (values + branch + b_mid).astype(jnp.bfloat16)


def solution(mesh):
    torus = Mesh(
        mesh.devices.reshape(mesh.shape["clip"], 4, 16, mesh.shape["ta"]),
        ("clip", "ha_0", "ha_1", "ta"),
    )
    return jax.shard_map(
        body,
        mesh=torus,
        in_specs=(P("clip", HA_TA, None), P(), P(), P(), P(), P(), P()),
        out_specs=P(("clip", "ta"), HA, None, None),
        check_vma=False,
    )
```

profile of v0, /device:TPU:33, one launch (start us, length us, event | category | flops | bytes accessed | tf_op | source)
XLA Modules:
  0.0 134.4 jit_solution(4511558677117919821)
XLA Ops:
  0.0 1.0 reshape.124
  1.0 23.8 %all_to_all.15 = bf16[2,2,4096]{2,1,0:T(2,128)(2,1)S(1)} all-to-all(bf16[2,2,4096]{2,1,0:T(2,128)(2,1)S(1)} %reshape.124), channel_id=1, replica_groups=mesh['clip'=2,'ha_0'=4,'ha_1'=16,'ta'=2] {'ta'}, dimensions={0} | all-to-all | bytes 65536 | tf_op jit(solution)/shard_map/all_to_all | solution.py:107
  24.9 0.1 copy.14
  25.2 0.2 copy.15
  25.4 1.3 collective-permute-start
  26.7 5.7 %fusion.24 = (bf16[1,1,3,384,384]{4,3,2,1,0:T(8,128)(2,1)}, bf16[1,1,3,384,384]{4,3,2,1,0:T(8,128)(2,1)}, bf16[1,1,3,384,384]{4,3,2,1,0:T(8,128)(2,1)}, bf16[1,1...) fusion(bf16[3,3,3,384,384]{4,3,2,1,0:T(8,128)(2,1)} %param.12), kind=kLoop, calls=%fused_computation.93 | loop fusion | bytes 15925248 | tf_op jit(solution)/shard_map/slice | solution.py:85
  32.8 1.3 collective-permute-start.2
  34.1 4.0 %collective-permute-start.1 = (bf16[8,2,128,16]{2,3,1,0:T(8,128)(2,1)S(1)}, bf16[8,2,128,16]{2,3,1,0:T(8,128)(2,1)S(1)}, u32[]{:S(2)}, u32[]{:S(2)}) collective-permute-start(bf16[8,2,128,16]{2,3,1,0:T(8,128)(2,1)S(1)} %pad_maximum_fusion.11), channel_id=1, source_target_pairs={{0,2},{2,4},{4,6},{6,8},{8,10},{10,12},{12,14},{14,16},{16,18},{18... | collective-permute-start | bytes 196616 | tf_op jit(solution)/shard_map/ppermute | solution.py:32
  38.2 1.2 collective-permute-done.1
  41.8 1.0 copy.18
  42.8 3.2 %reshape.112 = bf16[3072,432]{0,1:T(8,128)(2,1)} reshape(bf16[6,4,128,432]{2,1,0,3:T(4,128)(2,1)S(1)} %copy.18) | data formatting | bytes 5308416 | tf_op jit(solution)/shard_map/reshape | solution.py:60
  46.0 3.6 %add_convert_fusion = bf16[3072,384]{1,0:T(8,128)(2,1)S(1)} fusion(bf16[3072,432]{0,1:T(8,128)(2,1)} %reshape.112, bf16[432,384]{1,0:T(8,128)(2,1)S(1)} %bitcast.49, f32[384]{0:T(512)S(1)} %copy-done.14), kind=kOutput, calls=%fused_computation.1 | convolution fusion | flops 1021575168 | bytes 5346816 | tf_op jit(solution)/shard_map/dot_general | solution.py:61
  49.7 0.3 convert_reduce_fusion
  50.5 14.6 %all-reduce.3 = (f32[32]{0:T(128)S(1)}, f32[32]{0:T(128)S(1)}) all-reduce(f32[32]{0:T(128)S(1)} %reduce_sum.37, f32[32]{0:T(128)S(1)} %reduce_sum.25), channel_id=1, replica_groups=mesh['clip'=2,'ha_0'=4,'ha_1'=16,'ta'=2] {'ha_0'}, use_global_device_ids=true, to_apply=%region_7.8 | all-reduce | flops 64 | bytes 512 | tf_op jit(solution)/shard_map/psum | solution.py:39
  65.1 20.1 %all-reduce.2 = (f32[32]{0:T(128)S(1)}, f32[32]{0:T(128)S(1)}) all-reduce(f32[32]{0:T(128)S(1)} %get-tuple-element.9, f32[32]{0:T(128)S(1)} %get-tuple-element.10), channel_id=1, replica_groups=mesh['clip'=2,'ha_0'=4,'ha_1'=16,'ta'=2] {'ha_1'}, use_global_device_ids=true, to_apply=%region_8.9 | all-reduce | flops 64 | bytes 512 | tf_op jit(solution)/shard_map/psum | solution.py:39
  85.2 13.9 %all-reduce.4 = (f32[32]{0:T(128)S(1)}, f32[32]{0:T(128)S(1)}) all-reduce(f32[32]{0:T(128)S(1)} %get-tuple-element.7, f32[32]{0:T(128)S(1)} %get-tuple-element.8), channel_id=1, replica_groups=mesh['clip'=2,'ha_0'=4,'ha_1'=16,'ta'=2] {'ta'}, use_global_device_ids=true, to_apply=%region_9.10 | all-reduce | flops 64 | bytes 512 | tf_op jit(solution)/shard_map/psum | solution.py:39
  99.5 1.9 %fusion = bf16[6,4,128,384]{3,2,1,0:T(8,128)(2,1)S(1)} fusion(bf16[6,4,128,384]{3,2,1,0:T(8,128)(2,1)S(1)} %bitcast.53, f32[384]{0:T(512)S(1)} %copy-done.11, f32[384]{0:T(512)S(1)} %copy-done.12, f32[384]{0:T(512)S(1)} %mul.42, f32[384]{0:T(512)S(1)} %sub.21, pred[6,4]{1,0:T(8,128)(4,1)S(1)} %and_and_fusion), kind=kLoop, calls=%fused_computation.5 | loop fusion | flops 12976128 | bytes 4724760 | tf_op jit(solution)/shard_map/jit(_where)/select_n | solution.py:134
  101.4 3.5 %pad_slice_fusion.18 = (bf16[4,2,128,384]{3,2,1,0:T(8,128)(2,1)S(1)}, bf16[4,2,128,384]{3,2,1,0:T(8,128)(2,1)S(1)}, bf16[4,2,128,384]{3,2,1,0:T(8,128)(2,1)S(1)}...) fusion(bf16[6,4,128,384]{3,2,1,0:T(8,128)(2,1)S(1)} %fusion), kind=kLoop, calls=%fused_computation.75 | loop fusion | bytes 13369344 | tf_op jit(solution)/shard_map/slice | solution.py:74
  104.9 0.7 fusion.25
  105.6 3.8 %pad_slice_fusion.19 = (bf16[4,2,128,384]{3,2,1,0:T(8,128)(2,1)S(1)}, bf16[4,2,128,384]{3,2,1,0:T(8,128)(2,1)S(1)}, bf16[4,2,128,384]{3,2,1,0:T(8,128)(2,1)S(1)}...) fusion(bf16[6,4,128,384]{3,2,1,0:T(8,128)(2,1)S(1)} %fusion), kind=kLoop, calls=%fused_computation.76 | loop fusion | bytes 11010048 | tf_op jit(solution)/shard_map/slice | solution.py:74
  109.4 0.3 pad_maximum_fusion.7
  109.8 0.9 copy-done.10
  110.6 1.4 %fusion.33 = f32[1024,384]{1,0:T(8,128)S(1)} fusion(bf16[1024,1152]{1,0:T(8,128)(2,1)S(1)} %bitcast.55, bf16[1152,384]{1,0:T(8,128)(2,1)S(1)} %bitcast.72), kind=kOutput, calls=%fused_computation.102 | convolution fusion | flops 905969664 | bytes 4816896 | tf_op jit(solution)/shard_map/dot_general | solution.py:83
  112.1 0.3 pad_maximum_fusion.6
  112.4 0.9 copy-done.9
  113.2 1.4 %fusion.32 = f32[1024,384]{1,0:T(8,128)S(1)} fusion(bf16[1024,1152]{1,0:T(8,128)(2,1)S(1)} %bitcast.56, bf16[1152,384]{1,0:T(8,128)(2,1)S(1)} %bitcast.71), kind=kOutput, calls=%fused_computation.101 | convolution fusion | flops 905969664 | bytes 4816896 | tf_op jit(solution)/shard_map/dot_general | solution.py:83
  114.7 0.3 pad_maximum_fusion.5
  115.0 0.9 copy-done.8
  115.8 1.4 %fusion.31 = f32[1024,384]{1,0:T(8,128)S(1)} fusion(bf16[1024,1152]{1,0:T(8,128)(2,1)S(1)} %bitcast.57, bf16[1152,384]{1,0:T(8,128)(2,1)S(1)} %bitcast.70), kind=kOutput, calls=%fused_computation.100 | convolution fusion | flops 905969664 | bytes 4816896 | tf_op jit(solution)/shard_map/dot_general | solution.py:83
  117.3 0.3 pad_maximum_fusion.4
  117.6 0.9 copy-done.7
  118.4 1.4 %fusion.30 = f32[1024,384]{1,0:T(8,128)S(1)} fusion(bf16[1024,1152]{1,0:T(8,128)(2,1)S(1)} %bitcast.58, bf16[1152,384]{1,0:T(8,128)(2,1)S(1)} %bitcast.69), kind=kOutput, calls=%fused_computation.99 | convolution fusion | flops 905969664 | bytes 4816896 | tf_op jit(solution)/shard_map/dot_general | solution.py:83
  119.9 0.3 pad_maximum_fusion.3
  120.2 0.9 copy-done.6
  121.0 1.4 %fusion.29 = f32[1024,384]{1,0:T(8,128)S(1)} fusion(bf16[1024,1152]{1,0:T(8,128)(2,1)S(1)} %bitcast.59, bf16[1152,384]{1,0:T(8,128)(2,1)S(1)} %bitcast.68), kind=kOutput, calls=%fused_computation.98 | convolution fusion | flops 905969664 | bytes 4816896 | tf_op jit(solution)/shard_map/dot_general | solution.py:83
  122.5 0.3 pad_maximum_fusion.2
  122.8 0.9 copy-done.5
  123.7 1.4 %fusion.28 = f32[1024,384]{1,0:T(8,128)S(1)} fusion(bf16[1024,1152]{1,0:T(8,128)(2,1)S(1)} %bitcast.60, bf16[1152,384]{1,0:T(8,128)(2,1)S(1)} %bitcast.67), kind=kOutput, calls=%fused_computation.97 | convolution fusion | flops 905969664 | bytes 4816896 | tf_op jit(solution)/shard_map/dot_general | solution.py:83
  125.1 0.3 pad_maximum_fusion
  125.4 0.9 copy-done.4
  126.3 1.4 %fusion.26 = f32[1024,384]{1,0:T(8,128)S(1)} fusion(bf16[1024,1152]{1,0:T(8,128)(2,1)S(1)} %bitcast.61, bf16[1152,384]{1,0:T(8,128)(2,1)S(1)} %bitcast.66), kind=kOutput, calls=%fused_computation.95 | convolution fusion | flops 905969664 | bytes 4816896 | tf_op jit(solution)/shard_map/dot_general | solution.py:83
  127.7 0.3 pad_maximum_fusion.1
  128.0 0.9 copy-done.3
  128.9 1.4 %fusion.27 = f32[1024,384]{1,0:T(8,128)S(1)} fusion(bf16[1024,1152]{1,0:T(8,128)(2,1)S(1)} %bitcast.62, bf16[1152,384]{1,0:T(8,128)(2,1)S(1)} %bitcast.65), kind=kOutput, calls=%fused_computation.96 | convolution fusion | flops 905969664 | bytes 4816896 | tf_op jit(solution)/shard_map/dot_general | solution.py:83
  130.3 0.3 pad_maximum_fusion.8
  130.6 0.9 copy-done.2
  131.5 1.8 %add_add_fusion = f32[1024,384]{1,0:T(8,128)S(1)} fusion(f32[1024,384]{1,0:T(8,128)S(1)} %fusion.33, f32[1024,384]{1,0:T(8,128)S(1)} %fusion.32, f32[1024,384]{1,0:T(8,128)S(1)} %fusion.31, f32[1024,384]{1,0:T(8,128)S(1)} %fusion.30, f32[1024,384]{1,0:T(8,128)S(1)} %fusion.29, f32[1024,384]{1,0:T(8,128)S(1)} %fusion.28, f32[1024,384]{1,0:T(8,128)S(1)} %fusion.26, ...), kind=kOutput, calls=%fused_computation.18 | convolution fusion | flops 909115392 | bytes 17399808 | tf_op jit(solution)/shard_map/dot_general | solution.py:83
  133.3 1.1 fusion.3
  (70 shorter events, 3.7 us)
Async XLA Ops:
  0.0 46.0 %copy-start = (bf16[3,3,3,16,384]{4,3,2,1,0:T(8,128)(2,1)S(1)}, bf16[3,3,3,16,384]{4,3,2,1,0:T(8,128)(2,1)}, u32[]{:S(2)}) copy-start(bf16[3,3,3,16,384]{4,3,2,1,0:T(8,128)(2,1)} %param.8) | copy-start | bytes 995332
  25.4 7.2 %collective-permute-start = (bf16[4,2,128,16]{3,2,1,0:T(8,128)(2,1)S(1)}, bf16[4,2,128,16]{3,2,1,0:T(8,128)(2,1)S(1)}, u32[]{:S(2)}, u32[]{:S(2)}) collective-permute-start(bf16[4,2,128,16]{3,2,1,0:T(8,128)(2,1)S(1)} %bitcast.63), channel_id=1, source_target_pairs={{0,1},{2,3},{4,5},{6,7},{8,9},{10,11},{12,13},{14,15},{16,17},{18,... | collective-permute-start | bytes 98312 | tf_op jit(solution)/shard_map/ppermute | solution.py:22
  32.8 5.4 %collective-permute-start.2 = (bf16[8,2,128,16]{2,3,1,0:T(8,128)(2,1)S(1)}, bf16[8,2,128,16]{2,3,1,0:T(8,128)(2,1)S(1)}, u32[]{:S(2)}, u32[]{:S(2)}) collective-permute-start(bf16[8,2,128,16]{2,3,1,0:T(8,128)(2,1)S(1)} %pad_maximum_fusion.11), channel_id=1, source_target_pairs={{2,0},{4,2},{6,4},{8,6},{10,8},{12,10},{14,12},{16,14},{18,16},{20... | collective-permute-start | bytes 196616 | tf_op jit(solution)/shard_map/ppermute | solution.py:33
  34.1 5.4 %collective-permute-start.1 = (bf16[8,2,128,16]{2,3,1,0:T(8,128)(2,1)S(1)}, bf16[8,2,128,16]{2,3,1,0:T(8,128)(2,1)S(1)}, u32[]{:S(2)}, u32[]{:S(2)}) collective-permute-start(bf16[8,2,128,16]{2,3,1,0:T(8,128)(2,1)S(1)} %pad_maximum_fusion.11), channel_id=1, source_target_pairs={{0,2},{2,4},{4,6},{6,8},{8,10},{10,12},{12,14},{14,16},{16,18},{18... | collective-permute-start | bytes 196616 | tf_op jit(solution)/shard_map/ppermute | solution.py:32
  42.8 3.2 %copy-start.14 = (f32[384]{0:T(512)S(1)}, f32[384]{0:T(512)}, u32[]{:S(2)}) copy-start(f32[384]{0:T(512)} %param.9) | copy-start | bytes 4612
  46.0 53.4 %copy-start.11 = (f32[384]{0:T(512)S(1)}, f32[384]{0:T(512)}, u32[]{:S(2)}) copy-start(f32[384]{0:T(512)} %param.11) | copy-start | bytes 4612
  46.0 53.4 %copy-start.12 = (f32[384]{0:T(512)S(1)}, f32[384]{0:T(512)}, u32[]{:S(2)}) copy-start(f32[384]{0:T(512)} %param.10) | copy-start | bytes 4612
  109.4 1.2 copy-start.10
  112.0 1.2 copy-start.9
  114.7 1.2 copy-start.8
  117.3 1.2 copy-start.7
  119.9 1.2 copy-start.6
  122.5 1.2 copy-start.5
  125.1 1.2 copy-start.4
  127.7 1.2 copy-start.3
  130.3 1.2 copy-start.2
  131.5 1.8 %copy-start.13 = (f32[384]{0:T(512)S(1)}, f32[384]{0:T(512)}, u32[]{:S(2)}) copy-start(f32[384]{0:T(512)} %param.13) | copy-start | bytes 4612
  131.5 2.9 %copy-start.1 = (bf16[3,3,3,16,384]{4,3,2,1,0:T(8,128)(2,1)S(1)}, bf16[3,3,3,16,384]{4,3,2,1,0:T(8,128)(2,1)}, u32[]{:S(2)}) copy-start(bf16[3,3,3,16,384]{4,3,2,1,0:T(8,128)(2,1)} %param.8) | copy-start | bytes 995332
where the time goes:
time: 135 us; the launch traced here: 134 us
  blocking collectives  72.4 us (54%)
  local copies, waits for them, and re-layouts  30.2 us (22%)
  matrix products  16.9 us (13%)
  starting transfers between devices  6.65 us (5%)
  other arithmetic  6.34 us (5%)
    psum x3, blocking collectives, by_axis(): return functools.reduce(lax.psum, axes, value)  48.6 us
    all_to_all x1, blocking collectives, body(): lax.all_to_all(latent_tokens, 'ta', split_axis=0, concat_axis=1, tiled=True)  23.8 us
    dot_general x9, matrix products, middle_conv(): jnp.dot(slab, w_mid[frame_tap, row_tap].reshape(3 * channels, -1), prefer...  13.2 us
    unnamed x58, local copies, waits for them, and re-layouts  10.8 us
    slice x3, local copies, waits for them, and re-layouts, middle_conv(): padded[frame_tap:frame_tap + frames, row_tap:row_tap + rows, col_tap:col_...  8.05 us
    slice x1, local copies, waits for them, and re-layouts, middle_conv(): w_mid[frame_tap, row_tap].reshape(3 * channels, -1)  5.74 us
    ppermute x1, starting transfers between devices, extended_2(): before = lax.ppermute(last, axis, up)  4.03 us
    dot_general x1, matrix products, input_conv(): jnp.dot(stacked, w_in.reshape(stacked.shape[1], -1), preferred_element_ty...  3.62 us
  transfers between devices with their start and end apart: 3, of which 1 were waited for; matrix products, arithmetic and copies ran while one was open for 4% of the time, Pallas kernels for 0%

commit v1 on v0

v1 whole, which is shorter than its diff:
```python
import functools

import jax
import jax.numpy as jnp
from jax import lax
from jax.experimental import pallas as pl
from jax.experimental.pallas import tpu as pltpu
from jax.sharding import PartitionSpec as P

GROUPS = 32
RING_X = 4
RING_Z = 16
EPS = 1e-06
MESH = pl.DeviceIdType.MESH
BF16 = jnp.bfloat16
F32 = jnp.float32


def exchange_kernel(
    tok_ref, w_hbm, b_ref, gain_ref, shift_ref, mid_hbm,
    h_ref, stat_ref, main_ref, rest_ref,
    packed, field, patch, w_big, mid, mine, plane_in, plane_sum, ring_in, sel, one_hot, spread,
    w_sem, mid_sem, send_sem, recv_sem, plane_send, plane_recv, ring_send, ring_recv, know_x, know_z,
):
    ha, ta = lax.axis_index("ha"), lax.axis_index("ta")
    n_ha = lax.axis_size("ha")
    x, z = ha // RING_Z, ha % RING_Z
    channels = h_ref.shape[-1] // 2
    members = channels // GROUPS

    def near(dx, dz, flip):
        hx = (x + dx) % RING_X
        hz = (z + dz) % RING_Z
        return {"ha": hx * RING_Z + hz, "ta": 1 - ta if flip else ta}

    barrier = pltpu.get_barrier_semaphore()

    def greet(device):
        pl.semaphore_signal(barrier, inc=1, device_id=device, device_id_type=MESH)

    greet(near(0, 0, True))
    for flip in (False, True):
        for dz in (1, RING_Z - 1):
            greet(near(0, dz, flip))
        for dx in (1, RING_X - 1):
            greet(near(dx, 0, flip))
    after_edge = (z == RING_Z - 1) & (ha < n_ha - 1)
    before_edge = (z == 0) & (ha > 0)

    @pl.when(after_edge)
    def _():
        for t in (0, 1):
            greet({"ha": ha + 1, "ta": t})

    @pl.when(before_edge)
    def _():
        for t in (0, 1):
            greet({"ha": ha - 1, "ta": t})

    pairs = packed.shape[0]
    for g in range(pairs):
        packed[g] = jnp.concatenate(
            [tok_ref[2 * g].astype(F32), tok_ref[2 * g + 1].astype(F32)], axis=-1
        ).astype(BF16)
    half = packed.shape[1]
    own = pl.ds(ta * half, half)
    ring_edge = jnp.where(after_edge, 2, 0) + jnp.where(before_edge, 2, 0)
    pl.semaphore_wait(barrier, 9 + ring_edge)

    def tokens_to(to_ha, to_ta, place, slot):
        if to_ta:
            src, dst = packed, field.at[pl.ds(0, 4), place, own]
        else:
            src, dst = packed.at[pl.ds(0, 2)], field.at[pl.ds(2, 2), place, own]
        return pltpu.make_async_remote_copy(
            src, dst, send_sem.at[slot], recv_sem.at[place, ta],
            device_id={"ha": to_ha, "ta": to_ta}, device_id_type=MESH,
        )

    def tokens_from(place, src_ta, frames_8):
        there = pl.ds(src_ta * half, half)
        if frames_8:
            src, dst = packed, field.at[pl.ds(0, 4), place, there]
        else:
            src, dst = packed.at[pl.ds(0, 2)], field.at[pl.ds(2, 2), place, there]
        return pltpu.make_async_remote_copy(
            src, dst, send_sem.at[0], recv_sem.at[place, src_ta],
            device_id={"ha": ha, "ta": ta}, device_id_type=MESH,
        )

    @pl.when(ha < n_ha - 1)
    def _():
        tokens_to(ha + 1, 1, 0, 0).start()
        tokens_to(ha + 1, 0, 0, 1).start()

    @pl.when(ha > 0)
    def _():
        tokens_to(ha - 1, 1, 2, 2).start()
        tokens_to(ha - 1, 0, 2, 3).start()

    @pl.when(ta == 0)
    def _():
        tokens_to(ha, 1, 1, 4).start()

    @pl.when(ta == 1)
    def _():
        tokens_to(ha, 0, 1, 4).start()

    w_copies = []
    for high in (0, 1):
        for p in range(3):
            for b in (0, 1):
                w_copies.append(
                    pltpu.make_async_copy(
                        w_hbm.at[p],
                        w_big.at[high, p, pl.ds(high, 3), pl.ds(16 * b, 48), pl.ds(channels * b, channels)],
                        w_sem.at[len(w_copies)],
                    )
                )
    for copy in w_copies:
        copy.start()
    for high in (0, 1):
        w_big[high, :, 3 * (1 - high)] = jnp.zeros_like(w_big[high, :, 0])
        for p in range(3):
            for q in range(3):
                w_big[high, p, high + q, 48:64, :channels] = jnp.zeros((16, channels), BF16)
                w_big[high, p, high + q, 0:16, channels:] = jnp.zeros((16, channels), BF16)

    @pl.when(ta == 0)
    def _():
        field[0:2] = jnp.zeros_like(field[0:2])
        field[2:4, 1, own] = packed[0:2]

    @pl.when(ta == 1)
    def _():
        field[0:4, 1, own] = packed[0:4]

    @pl.when(ha == 0)
    def _():
        field[:, 0] = jnp.zeros_like(field[:, 0])

    @pl.when(ha == n_ha - 1)
    def _():
        field[:, 2] = jnp.zeros_like(field[:, 2])

    k = lax.broadcasted_iota(jnp.int32, sel.shape, 0)
    n = lax.broadcasted_iota(jnp.int32, sel.shape, 1)
    step, lane = k // 128, k % 128
    column = 2 * step + (lane // 16) % 2 - 1
    same = (lane // 32 == n // 64) & (lane % 16 == n % 16)
    sel[...] = jnp.where(same & (column == (n // 16) % 4), 1.0, 0.0).astype(BF16)
    k = lax.broadcasted_iota(jnp.int32, one_hot.shape, 0)
    n = lax.broadcasted_iota(jnp.int32, one_hot.shape, 1)
    low = jnp.where(n < GROUPS, n * members, channels + (n - GROUPS) * members)
    one_hot[...] = jnp.where((n < 2 * GROUPS) & (k >= low) & (k < low + members), 1.0, 0.0)
    k = lax.broadcasted_iota(jnp.int32, spread.shape, 0)
    n = lax.broadcasted_iota(jnp.int32, spread.shape, 1)
    low = jnp.where(k < GROUPS, k * members, channels + (k - GROUPS) * members)
    spread[...] = jnp.where((k < 2 * GROUPS) & (n >= low) & (n < low + members), 1.0, 0.0)

    def tell(sem, device):
        pl.semaphore_signal(sem, inc=1, device_id=device, device_id_type=MESH)

    tell(know_x, near(1, 0, False))
    tell(know_x, near(RING_X - 1, 0, False))
    tell(know_z.at[0], near(0, 1, False))
    tell(know_z.at[0], near(0, RING_Z - 1, False))
    for copy in w_copies:
        copy.wait()
    pl.semaphore_wait(know_z.at[0], 2)
    tell(know_z.at[1], near(0, 2, False))
    tell(know_z.at[1], near(0, RING_Z - 2, False))

    for frames_8 in (False, True):

        @pl.when(ta == int(frames_8))
        def _():
            tokens_from(1, int(not frames_8), frames_8).wait_recv()

            @pl.when(ha > 0)
            def _():
                for t in (0, 1):
                    tokens_from(0, t, frames_8).wait_recv()

            @pl.when(ha < n_ha - 1)
            def _():
                for t in (0, 1):
                    tokens_from(2, t, frames_8).wait_recv()

    tokens = field.shape[2]
    row = lax.broadcasted_iota(jnp.int32, (tokens, 128), 0)
    for i in range(3):
        stack = []
        for g in range(pairs):
            now = field[g, i].astype(F32)
            left = jnp.where(row == 0, 0.0, pltpu.roll(now, 1, 0))
            right = jnp.where(row == tokens - 1, 0.0, pltpu.roll(now, tokens - 1, 0))
            stack.append(jnp.concatenate([left, now, right], axis=-1).astype(BF16))
        moved = jnp.dot(jnp.concatenate(stack, axis=0), sel[...], preferred_element_type=F32)
        moved = moved.astype(BF16)
        for g in range(pairs):
            for f in (0, 1):
                patch[2 * g + f, :, 128 * i : 128 * i + 128] = moved[
                    g * tokens : (g + 1) * tokens, 128 * f : 128 * f + 128
                ]

    bias = b_ref[...].reshape(1, -1)
    bias = jnp.concatenate([bias, bias], axis=-1)

    def hidden_rows(y, first, frames):
        lanes = slice(0, 256) if y < 2 else slice(128, 384)
        high = y % 2
        total = bias
        for p in range(3):
            lhs = patch[first + p : first + p + frames, :, lanes].reshape(frames * tokens, 256)
            total = total + jnp.dot(
                lhs, w_big[high, p].reshape(256, 2 * channels), preferred_element_type=F32
            )
        return total.astype(BF16)

    sums = jnp.zeros((1, 2 * channels), F32)
    squares = jnp.zeros((1, 2 * channels), F32)
    for y in (1, 2):
        rows = hidden_rows(y, 2, 4)
        h_ref[2:6, y] = rows.reshape(4, tokens, 2 * channels)
        values = rows.astype(F32)
        sums = sums + jnp.sum(values, axis=0, keepdims=True)
        squares = squares + jnp.sum(values * values, axis=0, keepdims=True)
    folded = jnp.concatenate(
        [sums[:, :channels] + sums[:, channels:], squares[:, :channels] + squares[:, channels:]], axis=-1
    )
    mine[...] = jnp.dot(
        folded, one_hot[...], preferred_element_type=F32, precision=lax.Precision.HIGHEST
    )

    pl.semaphore_wait(know_z.at[1], 2)
    tell(know_z.at[2], near(0, 4, False))
    tell(know_z.at[2], near(0, RING_Z - 4, False))
    pl.semaphore_wait(know_x, 2)

    plane = []
    for dx in (2, 1, 3, 0):
        for flip in (0, 1):
            if dx or flip:
                slot = 2 * dx + flip - 1
                plane.append(
                    pltpu.make_async_remote_copy(
                        mine, plane_in.at[slot], plane_send.at[slot], plane_recv.at[slot],
                        device_id=near(dx, 0, bool(flip)), device_id_type=MESH,
                    )
                )
    for copy in plane:
        copy.start()

    h_ref[0:6, 0] = hidden_rows(0, 0, 6).reshape(6, tokens, 2 * channels)
    h_ref[0:6, 3] = hidden_rows(3, 0, 6).reshape(6, tokens, 2 * channels)
    for y in (1, 2):
        h_ref[0:2, y] = hidden_rows(y, 0, 2).reshape(2, tokens, 2 * channels)

    for p in range(2):
        pltpu.make_async_copy(mid_hbm.at[p], mid.at[p], mid_sem.at[p]).start()
    total = mine[...]
    for copy in plane:
        copy.wait_recv()
    for slot in range(plane_in.shape[0]):
        total = total + plane_in[slot]
    plane_sum[...] = total

    pl.semaphore_wait(know_z.at[2], 2)
    ring = []
    for d in sorted(range(1, RING_Z), key=lambda d: -min(d, RING_Z - d)):
        ring.append(
            pltpu.make_async_remote_copy(
                plane_sum, ring_in.at[d - 1], ring_send.at[d - 1], ring_recv.at[d - 1],
                device_id=near(0, d, False), device_id_type=MESH,
            )
        )
    for copy in ring:
        copy.start()


    wide = main_ref.shape[2]
    rest = channels - wide

    def fetch(p):
        return pltpu.make_async_copy(mid_hbm.at[p], mid.at[p % 2], mid_sem.at[p % 2])

    def bank(tap_0, tap_1, tap_2):
        ends = tap_0 + tap_2
        return tap_0, 0.5 * (ends + tap_1), 0.5 * (ends - tap_1), tap_2

    for i in range(16):
        rest_ref[i, 3 * channels :, :rest] = jnp.zeros((channels, rest), BF16)
        rest_ref[i, :channels, rest:] = jnp.zeros((channels, rest), BF16)
    for p in range(3):
        fetch(p).wait()

        def transform(step, carry):
            at = pl.multiple_of(step * 16, 16)
            for part in range(channels // 128):
                lanes = slice(128 * part, 128 * part + 128)
                taps = [
                    [mid[p % 2, q, r, pl.ds(at, 16), lanes].astype(F32) for r in range(3)] for q in range(3)
                ]
                by_row = [bank(*[taps[q][r] for q in range(3)]) for r in range(3)]
                for i in range(4):
                    for k, value in enumerate(bank(*[by_row[r][i] for r in range(3)])):
                        value = value.astype(BF16)
                        if 128 * part < wide:
                            main_ref[4 * i + k, pl.ds(at + p * channels, 16), lanes] = value
                        else:
                            rest_ref[4 * i + k, pl.ds(at + p * channels, 16), :rest] = value
                            rest_ref[4 * i + k, pl.ds(at + (p + 1) * channels, 16), rest:] = value
            return carry

        lax.fori_loop(0, channels // 16, transform, 0)
        if p == 0:
            fetch(2).start()

    @pl.when(ha < n_ha - 1)
    def _():
        tokens_to(ha + 1, 1, 0, 0).wait_send()
        tokens_to(ha + 1, 0, 0, 1).wait_send()

    @pl.when(ha > 0)
    def _():
        tokens_to(ha - 1, 1, 2, 2).wait_send()
        tokens_to(ha - 1, 0, 2, 3).wait_send()

    @pl.when(ta == 0)
    def _():
        tokens_to(ha, 1, 1, 4).wait_send()

    @pl.when(ta == 1)
    def _():
        tokens_to(ha, 0, 1, 4).wait_send()

    for copy in plane:
        copy.wait_send()

    for copy in ring:
        copy.wait_recv()
    for slot in range(ring_in.shape[0]):
        total = total + ring_in[slot]
    for copy in ring:
        copy.wait_send()

    count = n_ha * lax.axis_size("ta") * 4 * 2 * 2 * tokens * members
    spread_out = jnp.dot(
        total * (1.0 / count), spread[...], preferred_element_type=F32, precision=lax.Precision.HIGHEST
    )
    mean, square = spread_out[:, :channels], spread_out[:, channels:]
    var = jnp.maximum(square - mean * mean, 0.0)
    scale = lax.rsqrt(var + EPS) * gain_ref[...].reshape(1, -1)
    stat_ref[0:1] = 0.5 * scale
    stat_ref[1:2] = 0.5 * (shift_ref[...].reshape(1, -1) - mean * scale)


def decode_kernel(h_ref, stat_ref, main_ref, rest_ref, b_ref, out_ref, planes, acc, rows_f32):
    ha, ta = lax.axis_index("ha"), lax.axis_index("ta")
    n_ha = lax.axis_size("ha")
    frames_in, rows_in, tokens, width = h_ref.shape
    channels = width // 2
    frames, rows = frames_in - 2, rows_in - 2
    wide = main_ref.shape[2]
    rest = channels - wide
    place = lax.broadcasted_iota(jnp.int32, (tokens, 128), 0)

    def activate(f, carry):
        inside = [
            (f >= 2 - 2 * ta) & (ha * rows + y >= 1) & (ha * rows + y <= n_ha * rows) for y in range(rows_in)
        ]
        for part in range(channels // 128):
            lanes = slice(128 * part, 128 * part + 128)
            scale, shift = stat_ref[0:1, lanes], stat_ref[1:2, lanes]
            by_column = []
            for y in range(rows_in):
                row_scale = jnp.where(inside[y], scale, 0.0)
                row_shift = jnp.where(inside[y], shift, 0.0)

                def active(b):
                    lo = b * channels + 128 * part
                    value = h_ref[f, y, :, lo : lo + 128].astype(F32) * row_scale + row_shift
                    return value + value * jnp.tanh(value)

                even, odd = active(0), active(1)
                before = jnp.where(place == 0, 0.0, pltpu.roll(odd, 1, 0)).astype(BF16)
                after = jnp.where(place == tokens - 1, 0.0, pltpu.roll(even, tokens - 1, 0)).astype(BF16)
                even, odd = even.astype(BF16), odd.astype(BF16)
                by_column.append((before - odd, even + odd, odd - even, even - after))
            for k in range(4):
                y0, y1, y2, y3 = [by_column[y][k] for y in range(4)]
                for i, value in enumerate((y0 - y2, y1 + y2, y2 - y1, y1 - y3)):
                    planes[4 * i + k, f, :, lanes] = value
        return carry

    lax.fori_loop(0, frames_in, activate, 0)

    signs = ((1, 1, 1, 0), (0, 1, -1, -1))
    first = [[True, True], [True, True]]
    for i in range(4):
        for k in range(4):
            at = 4 * i + k
            lhs = jnp.concatenate([planes[at, p : p + frames] for p in range(3)], axis=-1)
            lhs = lhs.reshape(frames * tokens, 3 * channels)
            product = jnp.dot(lhs, main_ref[at], preferred_element_type=F32)
            lhs = jnp.concatenate(
                [
                    jnp.concatenate([planes[at, t + p] for p in range(4)], axis=-1)
                    for t in range(0, frames, 2)
                ],
                axis=0,
            )
            other = jnp.dot(lhs, rest_ref[at], preferred_element_type=F32)
            for y in (0, 1):
                for b in (0, 1):
                    sign = signs[y][i] * signs[b][k]
                    if not sign:
                        continue
                    for f in range(frames):
                        one = product[f * tokens : (f + 1) * tokens]
                        two = other[f // 2 * tokens : (f // 2 + 1) * tokens, rest * (f % 2) : rest * (f % 2) + rest]
                        for value, lanes in ((one, slice(0, wide)), (two, slice(wide, channels))):
                            value = value if sign > 0 else -value
                            if not first[y][b]:
                                value = acc[y, b, f, :, lanes] + value
                            acc[y, b, f, :, lanes] = value
                    first[y][b] = False
    bias = b_ref[...].reshape(1, -1)
    for f in range(frames):
        for y in range(rows):
            for b in (0, 1):
                hidden = h_ref[f + 2, y + 1, :, b * channels : (b + 1) * channels].astype(F32)
                total = acc[y, b, f] + hidden + bias
                for part in range(channels // 128):
                    rows_f32[part, pl.ds(b, tokens, stride=2)] = total[:, 128 * part : 128 * part + 128]
            for part in range(channels // 128):
                out_ref[f, y, :, 128 * part : 128 * part + 128] = rows_f32[part].astype(BF16)


def keep(value):
    return pltpu.with_memory_space_constraint(value, pltpu.HBM)


def body(latent_tokens, w_in, b_in, gn_gain, gn_shift, w_mid, b_mid):
    frames_all, half, token_lanes = latent_tokens.shape
    channels = w_in.shape[-1]
    tokens = 2 * half
    wide = channels // 256 * 256
    rest = channels - wide
    vmem = pl.BlockSpec(memory_space=pltpu.VMEM)
    hbm = pl.BlockSpec(memory_space=pltpu.HBM)
    hidden, stats, main, other = pl.pallas_call(
        exchange_kernel,
        out_shape=(
            jax.ShapeDtypeStruct((6, 4, tokens, 2 * channels), BF16),
            jax.ShapeDtypeStruct((2, channels), F32),
            jax.ShapeDtypeStruct((16, 3 * channels, wide), BF16),
            jax.ShapeDtypeStruct((16, 4 * channels, 2 * rest), BF16),
        ),
        in_specs=[vmem, hbm, vmem, vmem, vmem, hbm],
        out_specs=(vmem, vmem, vmem, vmem),
        scratch_shapes=[
            pltpu.VMEM((4, half, 128), BF16),
            pltpu.VMEM((4, 3, tokens, 128), BF16),
            pltpu.VMEM((8, tokens, 384), BF16),
            pltpu.VMEM((2, 3, 4, 64, 2 * channels), BF16),
            pltpu.VMEM((2, 3, 3, channels, channels), BF16),
            pltpu.VMEM((1, 128), F32),
            pltpu.VMEM((7, 1, 128), F32),
            pltpu.VMEM((1, 128), F32),
            pltpu.VMEM((RING_Z - 1, 1, 128), F32),
            pltpu.VMEM((384, 256), BF16),
            pltpu.VMEM((2 * channels, 128), F32),
            pltpu.VMEM((128, 2 * channels), F32),
            pltpu.SemaphoreType.DMA((12,)),
            pltpu.SemaphoreType.DMA((2,)),
            pltpu.SemaphoreType.DMA((5,)),
            pltpu.SemaphoreType.DMA((3, 2)),
            pltpu.SemaphoreType.DMA((7,)),
            pltpu.SemaphoreType.DMA((7,)),
            pltpu.SemaphoreType.DMA((RING_Z - 1,)),
            pltpu.SemaphoreType.DMA((RING_Z - 1,)),
            pltpu.SemaphoreType.REGULAR,
            pltpu.SemaphoreType.REGULAR((3,)),
        ],
        compiler_params=pltpu.CompilerParams(
            collective_id=0, has_side_effects=True, vmem_limit_bytes=16 * 2**20
        ),
        name="exchange",
    )(keep(latent_tokens), keep(w_in.reshape(3, 3, -1, channels)), keep(b_in), keep(gn_gain), keep(gn_shift), keep(w_mid))
    return pl.pallas_call(
        decode_kernel,
        out_shape=jax.ShapeDtypeStruct((4, 2, 2 * tokens, channels), BF16),
        in_specs=[vmem, vmem, vmem, vmem, vmem],
        out_specs=vmem,
        scratch_shapes=[
            pltpu.VMEM((16, 6, tokens, channels), BF16),
            pltpu.VMEM((2, 2, 4, tokens, channels), F32),
            pltpu.VMEM((channels // 128, 2 * tokens, 128), F32),
        ],
        compiler_params=pltpu.CompilerParams(vmem_limit_bytes=16 * 2**20),
        name="decode",
    )(hidden, stats, main, other, b_mid)


def solution(mesh):
    return jax.shard_map(
        body,
        mesh=mesh,
        in_specs=(P("clip", ("ha", "ta"), None), P(), P(), P(), P(), P(), P()),
        out_specs=P(("clip", "ta"), "ha", None, None),
        check_vma=False,
    )
```

time: 135 us -> 49.5 us (0.37)
  blocking collectives: 72.4 us -> 0 us
  Pallas kernels: 0 us -> 48.5 us
  local copies, waits for them, and re-layouts: 30.2 us -> 0.68 us
  matrix products: 16.9 us -> 0 us
  starting transfers between devices: 6.65 us -> 0 us
  other arithmetic: 6.34 us -> 0 us
    psum x3 -> x0, blocking collectives: 48.6 us -> none  [by_axis(): return functools.reduce(lax.psum, axes, value)]
    pallas_call x0 -> x2, Pallas kernels: none -> 48.5 us  [the longest x1 40.3 us: body(): pl.pallas_call(exchange_kernel, out_shape=(jax.ShapeDtypeStruct((6, 4, to...]
    all_to_all x1 -> x0, blocking collectives: 23.8 us -> none  [body(): lax.all_to_all(latent_tokens, 'ta', split_axis=0, concat_axis=1, tiled=True)]
    dot_general x10 -> x0, matrix products: 16.9 us -> none  [the longest x9 13.2 us: middle_conv(): jnp.dot(slab, w_mid[frame_tap, row_tap].reshape(3 * channels, -1), prefer...]
    slice x5 -> x0, local copies, waits for them, and re-layouts: 13.9 us -> none  [the longest x3 8.05 us: middle_conv(): padded[frame_tap:frame_tap + frames, row_tap:row_tap + rows, col_tap:col_...]
    unnamed x58 -> x2, local copies, waits for them, and re-layouts: 10.8 us -> 0.68 us
    ppermute x3 -> x0, starting transfers between devices: 6.65 us -> none  [the longest x1 4.03 us: extended_2(): before = lax.ppermute(last, axis, up)]
    reshape x3 -> x0, local copies, waits for them, and re-layouts: 3.4 us -> none  [the longest x1 3.17 us: input_conv(): stacked = jnp.concatenate(pieces, axis=-1).reshape(frames * rows * cols, -1)]
  transfers between devices with their start and end apart: 3 -> 0, of which waited for: 1 -> 0; matrix products, arithmetic and copies ran while one was open for 4% -> 0% of each run, Pallas kernels for 0% -> 0%
where the time goes in v1:
time: 49.5 us; the launch traced here: 49.2 us
  Pallas kernels  48.5 us (98%)
  local copies, waits for them, and re-layouts  0.68 us (1%)
    pallas_call x1, Pallas kernels, body(): pl.pallas_call(exchange_kernel, out_shape=(jax.ShapeDtypeStruct((6, 4, to...  40.3 us
    pallas_call x1, Pallas kernels, body(): pl.pallas_call(decode_kernel, out_shape=jax.ShapeDtypeStruct((4, 2, 2 * t...  8.26 us

profile of v1, /device:TPU:33, one launch (start us, length us, event | category | flops | bytes accessed | tf_op | source)
XLA Modules:
  0.0 49.2 jit_solution(12499410467744245339)
XLA Ops:
  0.0 40.3 %exchange.1 = (bf16[6,4,64,768]{3,2,1,0:T(8,128)(2,1)S(1)}, f32[2,384]{1,0:T(2,128)S(1)}, bf16[16,1152,256]{2,1,0:T(8,128)(2,1)S(1)}, bf16[16,1536,256]{2,1,0:T(8,128)(2,1)S(1)}) custom-call(bf16[8,32,64]{2,1,0:T(8,128)(2,1)} %tok_ref.1, bf16[3,3,48,384]{3,2,1,0:T(8,128)(2,1)} %bitcast.1, f32[384]{0:T(512)} %b_ref.2, f32[384]{0:T(512)} %gain_ref.1, ...), custom_call_target="tpu_custom_call" | custom-call | tf_op jit(solution)/shard_map/exchange/pallas_call | solution.py:453
  40.3 0.0 copy-start
  40.3 0.7 %copy-done = f32[384]{0:T(512)S(1)} copy-done((f32[384]{0:T(512)S(1)}, f32[384]{0:T(512)}, u32[]{:S(2)}) %copy-start) | copy-done | bytes 1560
  41.0 8.3 %decode.1 = bf16[4,2,128,384]{3,2,1,0:T(8,128)(2,1)} custom-call(bf16[6,4,64,768]{3,2,1,0:T(8,128)(2,1)S(1)} %get-tuple-element.9.h_ref, f32[2,384]{1,0:T(2,128)S(1)} %get-tuple-element.10.stat_ref, bf16[16,1152,256]{2,1,0:T(8,128)(2,1)S(1)} %get-tuple-element.11.main_ref, bf16[16,1536,256]{2,1,0:T(8,128)(2,1)S(1)} %get-tuple-element.12.rest_ref, f32[384]{0:T(512)S(1)} %copy-done), custom_call_target="tpu_custom_call" | custom-call | tf_op jit(solution)/shard_map/decode/pallas_call | solution.py:492
Async XLA Ops:
  40.3 0.7 %copy-start = (f32[384]{0:T(512)S(1)}, f32[384]{0:T(512)}, u32[]{:S(2)}) copy-start(f32[384]{0:T(512)} %b_ref.3) | copy-start | bytes 4612

commit v2 on v1

v2 whole, which is shorter than its diff:
```python
import jax
import jax.numpy as jnp
from jax import lax
from jax.experimental import pallas as pl
from jax.experimental.pallas import tpu as pltpu
from jax.sharding import PartitionSpec as P

GROUPS = 32
RING_X = 4
RING_Z = 16
EPS = 1e-06
MESH = pl.DeviceIdType.MESH
BF16 = jnp.bfloat16
F32 = jnp.float32


def exchange_kernel(
    tok_hbm, w_hbm, b_hbm, gain_hbm, shift_hbm, b_mid_hbm, mid_hbm,
    h_ref, stat_ref, main_ref, rest_ref,
    tok, vectors, packed, field, patch, w_big, mid, mine, plane_in, plane_sum, ring_in, sel, member,
    tok_sem, vec_sem, w_sem, mid_sem, send_sem, recv_sem,
    plane_send, plane_recv, ring_send, ring_recv, know_x, know_all, know_first,
):
    ha, ta = lax.axis_index("ha"), lax.axis_index("ta")
    n_ha = lax.axis_size("ha")
    x, z = ha // RING_Z, ha % RING_Z
    channels = vectors.shape[1]
    members = channels // GROUPS
    parts = channels // 128

    def near(dx, dz, flip):
        hx = (x + dx) % RING_X
        hz = (z + dz) % RING_Z
        return {"ha": hx * RING_Z + hz, "ta": 1 - ta if flip else ta}
    barrier = pltpu.get_barrier_semaphore()

    def greet(device):
        pl.semaphore_signal(barrier, inc=1, device_id=device, device_id_type=MESH)

    last = RING_Z - 1

    @pl.when(ha < n_ha - 1)
    def _():
        for t in (0, 1):
            greet({"ha": ha + 1, "ta": t})

    @pl.when(ha > 0)
    def _():
        for t in (0, 1):
            greet({"ha": ha - 1, "ta": t})

    for flip in (False, True):
        for dx in (1, RING_X - 1):
            greet(near(dx, 0, flip))
    greet(near(0, 0, True))

    @pl.when(z == 0)
    def _():
        greet(near(0, last, False))

    for d in range(2, last):

        @pl.when((z >= 1) & (z + d <= last))
        def _():
            greet(near(0, d, False))

    tok_copy = pltpu.make_async_copy(tok_hbm, tok, tok_sem)
    tok_copy.start()
    w_copies = [
        pltpu.make_async_copy(
            w_hbm,
            w_big.at[high, :, pl.ds(high, 3), pl.ds(16 * b, 48), pl.ds(channels * b, channels)],
            w_sem.at[2 * high + b],
        )
        for high in (0, 1)
        for b in (0, 1)
    ]
    for copy in w_copies:
        copy.start()
    vector_copies = [
        pltpu.make_async_copy(ref, vectors.at[i], vec_sem.at[i])
        for i, ref in enumerate((b_hbm, gain_hbm, shift_hbm, b_mid_hbm))
    ]
    for copy in vector_copies:
        copy.start()

    wide = main_ref.shape[2]
    rest = channels - wide

    def fetch(p):
        return pltpu.make_async_copy(mid_hbm.at[p], mid.at[p], mid_sem.at[p])

    for p in range(3):
        fetch(p).start()

    def bank(tap_0, tap_1, tap_2):
        ends = tap_0 + tap_2
        return tap_0, 0.5 * (ends + tap_1), 0.5 * (ends - tap_1), tap_2

    def transform(p):
        fetch(p).wait()

        def rows(step, carry):
            at = pl.multiple_of(step * 16, 16)
            for part in range(parts):
                lanes = slice(128 * part, 128 * part + 128)
                taps = [[mid[p, q, r, pl.ds(at, 16), lanes].astype(F32) for r in range(3)] for q in range(3)]
                by_row = [bank(*[taps[q][r] for q in range(3)]) for r in range(3)]
                for i in range(4):
                    for k, value in enumerate(bank(*[by_row[r][i] for r in range(3)])):
                        value = value.astype(BF16)
                        if 128 * part < wide:
                            main_ref[4 * i + k, pl.ds(at + p * channels, 16), lanes] = value
                        else:
                            rest_ref[4 * i + k, pl.ds(at + p * channels, 16), :rest] = value
                            rest_ref[4 * i + k, pl.ds(at + (p + 1) * channels, 16), rest:] = value
            return carry

        lax.fori_loop(0, channels // 16, rows, 0)

    early = z < RING_Z // 2

    @pl.when(early)
    def _():
        transform(0)
        transform(1)
    tok_copy.wait()
    pairs = packed.shape[0]
    for g in range(pairs):
        packed[g] = jnp.concatenate([tok[2 * g].astype(F32), tok[2 * g + 1].astype(F32)], axis=-1).astype(BF16)
    half = packed.shape[1]
    own = pl.ds(ta * half, half)
    expected = (
        5
        + jnp.where(ha > 0, 2, 0)
        + jnp.where(ha < n_ha - 1, 2, 0)
        + jnp.maximum(z - 2, 0)
        + jnp.where(z == last, 1, 0)
    )
    pl.semaphore_wait(barrier, expected)
    def tokens_to(to_ha, to_ta, place, slot):
        if to_ta:
            src, dst = packed, field.at[pl.ds(0, 4), place, own]
        else:
            src, dst = packed.at[pl.ds(0, 2)], field.at[pl.ds(2, 2), place, own]
        return pltpu.make_async_remote_copy(
            src, dst, send_sem.at[slot], recv_sem.at[place, ta],
            device_id={"ha": to_ha, "ta": to_ta}, device_id_type=MESH,
        )

    def tokens_from(place, src_ta, frames_8):
        there = pl.ds(src_ta * half, half)
        if frames_8:
            src, dst = packed, field.at[pl.ds(0, 4), place, there]
        else:
            src, dst = packed.at[pl.ds(0, 2)], field.at[pl.ds(2, 2), place, there]
        return pltpu.make_async_remote_copy(
            src, dst, send_sem.at[0], recv_sem.at[place, src_ta],
            device_id={"ha": ha, "ta": ta}, device_id_type=MESH,
        )

    def each_token_copy(act):
        @pl.when(ha < n_ha - 1)
        def _():
            act(tokens_to(ha + 1, 1, 0, 0))
            act(tokens_to(ha + 1, 0, 0, 1))

        @pl.when(ha > 0)
        def _():
            act(tokens_to(ha - 1, 1, 2, 2))
            act(tokens_to(ha - 1, 0, 2, 3))

        @pl.when(ta == 0)
        def _():
            act(tokens_to(ha, 1, 1, 4))

        @pl.when(ta == 1)
        def _():
            act(tokens_to(ha, 0, 1, 4))

    each_token_copy(lambda copy: copy.start())

    def tell(sem, device):
        pl.semaphore_signal(sem, inc=1, device_id=device, device_id_type=MESH)

    tell(know_x, near(1, 0, False))
    tell(know_x, near(RING_X - 1, 0, False))

    def pass_first(where, onwards):
        @pl.when(where & (z >= 2))
        def _():
            pl.semaphore_wait(know_first, 1)

        @pl.when(where & (z >= 1) & onwards)
        def _():
            tell(know_first, near(0, 1, False))

    pass_first(early, True)
    middle = (z == RING_Z // 2) | (z == RING_Z // 2 + 1)

    @pl.when(z == last)
    def _():
        for d in range(1, RING_Z):
            tell(know_all, near(0, d, False))
    @pl.when(ta == 0)
    def _():
        field[0:2] = jnp.zeros_like(field[0:2])
        field[2:4, 1, own] = packed[0:2]

    @pl.when(ta == 1)
    def _():
        field[0:4, 1, own] = packed[0:4]

    @pl.when(ha == 0)
    def _():
        field[:, 0] = jnp.zeros_like(field[:, 0])

    @pl.when(ha == n_ha - 1)
    def _():
        field[:, 2] = jnp.zeros_like(field[:, 2])

    for high in (0, 1):
        w_big[high, :, 3 * (1 - high)] = jnp.zeros_like(w_big[high, :, 0])
        for p in range(3):
            for q in range(3):
                w_big[high, p, high + q, 48:64, :channels] = jnp.zeros((16, channels), BF16)
                w_big[high, p, high + q, 0:16, channels:] = jnp.zeros((16, channels), BF16)
    k = lax.broadcasted_iota(jnp.int32, sel.shape, 0)
    n = lax.broadcasted_iota(jnp.int32, sel.shape, 1)
    step, lane = k // 128, k % 128
    column = 2 * step + (lane // 16) % 2 - 1
    same = (lane // 32 == n // 64) & (lane % 16 == n % 16)
    sel[...] = jnp.where(same & (column == (n // 16) % 4), 1.0, 0.0).astype(BF16)
    k = lax.broadcasted_iota(jnp.int32, (channels, channels), 0)
    n = lax.broadcasted_iota(jnp.int32, (channels, channels), 1)
    member[...] = jnp.where(k // members == n // members, 1.0, 0.0).astype(BF16)
    for copy in vector_copies:
        copy.wait()
    for copy in w_copies:
        copy.wait()
    for frames_8 in (False, True):

        @pl.when(ta == int(frames_8))
        def _():
            tokens_from(1, int(not frames_8), frames_8).wait_recv()

            @pl.when(ha > 0)
            def _():
                for t in (0, 1):
                    tokens_from(0, t, frames_8).wait_recv()

            @pl.when(ha < n_ha - 1)
            def _():
                for t in (0, 1):
                    tokens_from(2, t, frames_8).wait_recv()
    tokens = field.shape[2]
    row = lax.broadcasted_iota(jnp.int32, (tokens, 128), 0)

    def patches(pairs_now):
        for i in range(3):
            stack = []
            for g in pairs_now:
                now = field[g, i].astype(F32)
                left = jnp.where(row == 0, 0.0, pltpu.roll(now, 1, 0))
                right = jnp.where(row == tokens - 1, 0.0, pltpu.roll(now, tokens - 1, 0))
                stack.append(jnp.concatenate([left, now, right], axis=-1).astype(BF16))
            moved = jnp.dot(jnp.concatenate(stack, axis=0), sel[...], preferred_element_type=F32)
            moved = moved.astype(BF16)
            for at, g in enumerate(pairs_now):
                for f in (0, 1):
                    patch[2 * g + f, i] = moved[at * tokens : (at + 1) * tokens, 128 * f : 128 * f + 128]

    patches((1, 2, 3))
    bias = vectors[0].reshape(1, -1)
    bias = jnp.concatenate([bias, bias], axis=-1)

    def hidden_rows(y, first, frames):
        low, high = y // 2, y % 2
        total = bias
        for p in range(3):
            lhs = [
                patch[first + p : first + p + frames, i].reshape(frames * tokens, 128) for i in (low, low + 1)
            ]
            lhs = jnp.concatenate(lhs, axis=-1)
            total = total + jnp.dot(
                lhs, w_big[high, p].reshape(256, 2 * channels), preferred_element_type=F32
            )
        total = total.astype(BF16).astype(F32)
        for n in range(2 * parts):
            part = total[:, 128 * n : 128 * n + 128]
            h_ref[first : first + frames, y, n] = part.reshape(frames, tokens, 128)
        return total

    sums = jnp.zeros((1, 2 * channels), F32)
    squares = jnp.zeros((1, 2 * channels), F32)
    for y in (1, 2):
        values = hidden_rows(y, 2, 4)
        sums = sums + jnp.sum(values, axis=0, keepdims=True)
        squares = squares + jnp.sum(values * values, axis=0, keepdims=True)
    for at, both in ((0, sums), (parts, squares)):
        one = both[:, :channels] + both[:, channels:]
        for part in range(parts):
            mine[at + part : at + part + 1] = one[:, 128 * part : 128 * part + 128]
    mine[2 * parts :] = jnp.zeros_like(mine[2 * parts :])
    pl.semaphore_wait(know_x, 2)
    plane = []
    for dx in (2, 1, 3, 0):
        for flip in (0, 1):
            if dx or flip:
                slot = 2 * dx + flip - 1
                plane.append(
                    pltpu.make_async_remote_copy(
                        mine, plane_in.at[slot], plane_send, plane_recv,
                        device_id=near(dx, 0, bool(flip)), device_id_type=MESH,
                    )
                )
    for copy in plane:
        copy.start()
    patches((0,))
    hidden_rows(0, 0, 6)
    hidden_rows(3, 0, 6)
    hidden_rows(1, 0, 2)
    hidden_rows(2, 0, 2)
    total = mine[...]
    all_plane = pltpu.make_async_remote_copy(
        plane_in, plane_in, plane_send, plane_recv, device_id=near(0, 0, True), device_id_type=MESH
    )
    all_plane.wait_recv()
    for slot in range(plane_in.shape[0]):
        total = total + plane_in[slot]
    plane_sum[...] = total
    def ring_copy(d):
        return pltpu.make_async_remote_copy(
            plane_sum, ring_in.at[d - 1], ring_send, ring_recv,
            device_id=near(0, d, False), device_id_type=MESH,
        )

    ring_copy(1).start()
    for d in range(2, RING_Z):

        @pl.when((z + d > RING_Z) | ((z == 1) & (d == last)))
        def _():
            ring_copy(d).start()

    pass_first(middle, z == RING_Z // 2)
    for d in range(2, last):

        @pl.when((early | middle) & (z + d == RING_Z))
        def _():
            ring_copy(d).start()
    for i in range(16):
        rest_ref[i, 3 * channels :, :rest] = jnp.zeros((channels, rest), BF16)
        rest_ref[i, :channels, rest:] = jnp.zeros((channels, rest), BF16)
    stat_ref[2:3] = vectors[3].reshape(1, -1)

    @pl.when(early)
    def _():
        transform(2)
    @pl.when(z < last)
    def _():
        pl.semaphore_wait(know_all, 1)

    for d in range(2, RING_Z):

        @pl.when((z + d <= last) | (jnp.logical_not(early | middle) & (z + d == RING_Z) & (z < last)))
        def _():
            ring_copy(d).start()
    @pl.when(jnp.logical_not(early))
    def _():
        for p in range(3):
            transform(p)
    each_token_copy(lambda copy: copy.wait_send())
    all_plane.wait_send()
    all_ring = pltpu.make_async_remote_copy(
        ring_in, ring_in, ring_send, ring_recv, device_id=near(0, 1, False), device_id_type=MESH
    )
    all_ring.wait_recv()
    for slot in range(ring_in.shape[0]):
        total = total + ring_in[slot]
    count = n_ha * lax.axis_size("ta") * 4 * 2 * 2 * tokens * members
    sums = jnp.concatenate([total[part : part + 1] for part in range(parts)], axis=-1)
    squares = jnp.concatenate([total[parts + part : parts + part + 1] for part in range(parts)], axis=-1)
    terms = []
    for value in (sums, squares):
        for _ in range(3):
            term = value.astype(BF16)
            terms.append(term.astype(F32))
            value = value - terms[-1]
    terms = jnp.concatenate(terms + [jnp.zeros((2, channels), F32)], axis=0).astype(BF16)
    shared = jnp.dot(terms, member[...], preferred_element_type=F32) * (1.0 / count)
    mean = shared[0:1] + shared[1:2] + shared[2:3]
    square = shared[3:4] + shared[4:5] + shared[5:6]
    var = jnp.maximum(square - mean * mean, 0.0)
    scale = lax.rsqrt(var + EPS) * vectors[1].reshape(1, -1)
    stat_ref[0:1] = 0.5 * scale
    stat_ref[1:2] = 0.5 * (vectors[2].reshape(1, -1) - mean * scale)
    all_ring.wait_send()


def decode_kernel(
    h_ref, stat_ref, main_ref, rest_ref, out_hbm,
    shifted, columns_wide, columns_rest, planes_wide, planes_rest, acc, rows_f32, out, out_sem,
):
    ha, ta = lax.axis_index("ha"), lax.axis_index("ta")
    n_ha = lax.axis_size("ha")
    frames_in, rows_in, pieces, tokens, _ = h_ref.shape
    parts = pieces // 2
    channels = 128 * parts
    frames, rows = frames_in - 2, rows_in - 2
    wide = main_ref.shape[2]
    rest = channels - wide
    for part in range(parts):
        for y in range(rows_in):
            shifted[part, y, 0, 8 + tokens :] = jnp.zeros((8, 128), F32)
            shifted[part, y, 1, :8] = jnp.zeros((8, 128), F32)

    def activate(f, carry):
        inside = [
            (f >= 2 - 2 * ta) & (ha * rows + y >= 1) & (ha * rows + y <= n_ha * rows) for y in range(rows_in)
        ]
        for y in range(rows_in):
            by_part = []
            for part in range(parts):
                lanes = slice(128 * part, 128 * part + 128)
                row_scale = jnp.where(inside[y], stat_ref[0:1, lanes], 0.0)
                row_shift = jnp.where(inside[y], stat_ref[1:2, lanes], 0.0)
                columns = []
                for b in (0, 1):
                    value = h_ref[f, y, b * parts + part] * row_scale + row_shift
                    value = value + value * jnp.tanh(value)
                    shifted[part, y, b, 8 : 8 + tokens] = value
                    columns.append(value)
                even, odd = columns
                before = shifted[part, y, 1, 7 : 7 + tokens]
                after = shifted[part, y, 0, 9 : 9 + tokens]
                by_part.append((before - odd, even + odd, odd - even, even - after))
            for k in range(4):
                value = jnp.concatenate([by_part[part][k] for part in range(wide // 128)], axis=-1)
                columns_wide[k, f, y] = value.astype(BF16)
                value = jnp.concatenate([by_part[part][k] for part in range(wide // 128, parts)], axis=-1)
                columns_rest[k, f, y] = value.astype(BF16)
        return carry

    lax.fori_loop(0, frames_in, activate, 0)

    def by_rows(i, k):
        one, two = ((0, 2), (1, 2), (2, 1), (1, 3))[i]
        for columns, planes in ((columns_wide, planes_wide), (columns_rest, planes_rest)):
            if i == 1:
                planes[k % 2] = columns[k, :, one] + columns[k, :, two]
            else:
                planes[k % 2] = columns[k, :, one] - columns[k, :, two]

    by_rows(0, 0)
    bias = stat_ref[2:3]
    copies = []

    def finish(y):
        for f in range(frames):
            for part in range(parts):
                lanes = slice(128 * part, 128 * part + 128)
                for b in (0, 1):
                    hidden = h_ref[f + 2, y + 1, b * parts + part]
                    rows_f32[y, f, part, pl.ds(b, tokens, stride=2)] = acc[y, b, f, part] + (
                        hidden + bias[:, lanes]
                    )
                out[f, y, :, lanes] = rows_f32[y, f, part].astype(BF16)
            copies.append(pltpu.make_async_copy(out.at[f, y], out_hbm.at[f, y], out_sem.at[frames * y + f]))
            copies[-1].start()

    signs = ((1, 1, 1, 0), (0, 1, -1, -1))
    first = [[True, True], [True, True]]
    for i in range(4):
        for k in range(4):
            at = 4 * i + k
            if at < 15:
                by_rows((at + 1) // 4, (at + 1) % 4)
            both = (planes_wide.at[k % 2], planes_rest.at[k % 2])
            lhs = [planes[p : p + frames] for p in range(3) for planes in both]
            lhs = jnp.concatenate(lhs, axis=-1).reshape(frames * tokens, 3 * channels)
            product = jnp.dot(lhs, main_ref[at], preferred_element_type=F32)
            lhs = [
                jnp.concatenate([planes[t + p] for p in range(4) for planes in both], axis=-1)
                for t in range(0, frames, 2)
            ]
            other = jnp.dot(jnp.concatenate(lhs, axis=0), rest_ref[at], preferred_element_type=F32)
            for y in (0, 1):
                for b in (0, 1):
                    sign = signs[y][i] * signs[b][k]
                    if not sign:
                        continue
                    for f in range(frames):
                        for part in range(parts):
                            if 128 * part < wide:
                                value = product[f * tokens : (f + 1) * tokens, 128 * part : 128 * part + 128]
                            else:
                                value = other[
                                    f // 2 * tokens : (f // 2 + 1) * tokens,
                                    rest * (f % 2) : rest * (f % 2) + rest,
                                ]
                            if first[y][b]:
                                acc[y, b, f, part] = value if sign > 0 else -value
                            elif sign > 0:
                                acc[y, b, f, part] = acc[y, b, f, part] + value
                            else:
                                acc[y, b, f, part] = acc[y, b, f, part] - value
                    first[y][b] = False
        if i == 2:
            finish(0)
    finish(1)
    for y in (0, 1):
        for f in range(frames):
            copies[frames * y + f].wait()


def keep(value):
    return pltpu.with_memory_space_constraint(value, pltpu.HBM)


def body(latent_tokens, w_in, b_in, gn_gain, gn_shift, w_mid, b_mid):
    half = latent_tokens.shape[1]
    channels = w_in.shape[-1]
    tokens = 2 * half
    wide = channels // 256 * 256
    rest = channels - wide
    parts = channels // 128
    vmem = pl.BlockSpec(memory_space=pltpu.VMEM)
    hbm = pl.BlockSpec(memory_space=pltpu.HBM)
    inputs = (latent_tokens, w_in.reshape(3, 3, -1, channels), b_in, gn_gain, gn_shift, b_mid, w_mid)
    prepared = pl.pallas_call(
        exchange_kernel,
        out_shape=(
            jax.ShapeDtypeStruct((6, 4, 2 * parts, tokens, 128), F32),
            jax.ShapeDtypeStruct((3, channels), F32),
            jax.ShapeDtypeStruct((16, 3 * channels, wide), BF16),
            jax.ShapeDtypeStruct((16, 4 * channels, 2 * rest), BF16),
        ),
        in_specs=[hbm] * len(inputs),
        out_specs=(vmem, vmem, vmem, vmem),
        scratch_shapes=[
            pltpu.VMEM(latent_tokens.shape, BF16),
            pltpu.VMEM((4, channels), F32),
            pltpu.VMEM((4, half, 128), BF16),
            pltpu.VMEM((4, 3, tokens, 128), BF16),
            pltpu.VMEM((8, 3, tokens, 128), BF16),
            pltpu.VMEM((2, 3, 4, 64, 2 * channels), BF16),
            pltpu.VMEM(w_mid.shape, BF16),
            pltpu.VMEM((8, 128), F32),
            pltpu.VMEM((7, 8, 128), F32),
            pltpu.VMEM((8, 128), F32),
            pltpu.VMEM((RING_Z - 1, 8, 128), F32),
            pltpu.VMEM((384, 256), BF16),
            pltpu.VMEM((channels, channels), BF16),
            pltpu.SemaphoreType.DMA,
            pltpu.SemaphoreType.DMA((4,)),
            pltpu.SemaphoreType.DMA((4,)),
            pltpu.SemaphoreType.DMA((3,)),
            pltpu.SemaphoreType.DMA((5,)),
            pltpu.SemaphoreType.DMA((3, 2)),
            pltpu.SemaphoreType.DMA,
            pltpu.SemaphoreType.DMA,
            pltpu.SemaphoreType.DMA,
            pltpu.SemaphoreType.DMA,
            pltpu.SemaphoreType.REGULAR,
            pltpu.SemaphoreType.REGULAR,
            pltpu.SemaphoreType.REGULAR,
        ],
        compiler_params=pltpu.CompilerParams(
            collective_id=0, has_side_effects=True, vmem_limit_bytes=20 * 2**20
        ),
        name="exchange",
    )(*[keep(value) for value in inputs])
    return pl.pallas_call(
        decode_kernel,
        out_shape=jax.ShapeDtypeStruct((4, 2, 2 * tokens, channels), BF16),
        in_specs=[vmem, vmem, vmem, vmem],
        out_specs=hbm,
        scratch_shapes=[
            pltpu.VMEM((parts, 4, 2, tokens + 16, 128), F32),
            pltpu.VMEM((4, 6, 4, tokens, wide), BF16),
            pltpu.VMEM((4, 6, 4, tokens, rest), BF16),
            pltpu.VMEM((2, 6, tokens, wide), BF16),
            pltpu.VMEM((2, 6, tokens, rest), BF16),
            pltpu.VMEM((2, 2, 4, parts, tokens, 128), F32),
            pltpu.VMEM((2, 4, parts, 2 * tokens, 128), F32),
            pltpu.VMEM((4, 2, 2 * tokens, channels), BF16),
            pltpu.SemaphoreType.DMA((8,)),
        ],
        compiler_params=pltpu.CompilerParams(vmem_limit_bytes=18 * 2**20),
        name="decode",
    )(*prepared)


def solution(mesh):
    return jax.shard_map(
        body,
        mesh=mesh,
        in_specs=(P("clip", ("ha", "ta"), None), P(), P(), P(), P(), P(), P()),
        out_specs=P(("clip", "ta"), "ha", None, None),
        check_vma=False,
    )
```

time: 49.5 us -> 46.2 us (0.933)
  Pallas kernels: 48.5 us -> 46.1 us
  local copies, waits for them, and re-layouts: 0.68 us -> 0 us
    pallas_call x1, Pallas kernels: 40.3 us -> 37.9 us  [body(): pl.pallas_call(exchange_kernel, out_shape=(jax.ShapeDtypeStruct((6, 4, 2...]
    unnamed x2 -> x0, local copies, waits for them, and re-layouts: 0.68 us -> none
where the time goes in v2:
time: 46.2 us; the launch traced here: 46.1 us
  Pallas kernels  46.1 us (100%)
    pallas_call x1, Pallas kernels, body(): pl.pallas_call(exchange_kernel, out_shape=(jax.ShapeDtypeStruct((6, 4, 2...  37.9 us
    pallas_call x1, Pallas kernels, body(): pl.pallas_call(decode_kernel, out_shape=jax.ShapeDtypeStruct((4, 2, 2 * t...  8.23 us

profile of v2, /device:TPU:33, one launch (start us, length us, event | category | flops | bytes accessed | tf_op | source)
XLA Modules:
  0.0 46.1 jit_solution(14664294401912939165)
XLA Ops:
  0.0 37.9 %exchange.1 = (f32[6,4,6,64,128]{4,3,2,1,0:T(8,128)S(1)}, f32[3,384]{1,0:T(4,128)S(1)}, bf16[16,1152,256]{2,1,0:T(8,128)(2,1)S(1)}, bf16[16,1536,256]{2,1,0:T(8,128)(2,1)S(1)}) custom-call(bf16[8,32,64]{2,1,0:T(8,128)(2,1)} %tok_hbm.1, bf16[3,3,48,384]{3,2,1,0:T(8,128)(2,1)} %bitcast.1, f32[384]{0:T(512)} %b_hbm.1, f32[384]{0:T(512)} %gain_hbm.1, ...), custom_call_target="tpu_custom_call" | custom-call | tf_op jit(solution)/shard_map/exchange/pallas_call | solution.py:530
  37.9 8.2 %decode.1 = bf16[4,2,128,384]{3,2,1,0:T(8,128)(2,1)} custom-call(f32[6,4,6,64,128]{4,3,2,1,0:T(8,128)S(1)} %get-tuple-element.9.h_ref, f32[3,384]{1,0:T(4,128)S(1)} %get-tuple-element.10.stat_ref, bf16[16,1152,256]{2,1,0:T(8,128)(2,1)S(1)} %get-tuple-element.11.main_ref, bf16[16,1536,256]{2,1,0:T(8,128)(2,1)S(1)} %get-tuple-element.12.rest_ref), custom_call_target="tpu_custom_call" | custom-call | tf_op jit(solution)/shard_map/decode/pallas_call | solution.py:573

commit v3 on v2

--- a/solution.py
+++ b/solution.py
@@ -8,6 +8,8 @@
 GROUPS = 32
 RING_X = 4
 RING_Z = 16
+LATE = 4
+EARLY = 4
 EPS = 1e-06
 MESH = pl.DeviceIdType.MESH
 BF16 = jnp.bfloat16
@@ -17,9 +19,11 @@
 def exchange_kernel(
     tok_hbm, w_hbm, b_hbm, gain_hbm, shift_hbm, b_mid_hbm, mid_hbm,
     h_ref, stat_ref, main_ref, rest_ref,
-    tok, vectors, packed, field, patch, w_big, mid, mine, plane_in, plane_sum, ring_in, sel, member,
-    tok_sem, vec_sem, w_sem, mid_sem, send_sem, recv_sem,
-    plane_send, plane_recv, ring_send, ring_recv, know_x, know_all, know_first,
+    tok, vectors, packed, field, patch, w_big, mid, mine, plane_in, plane_sum, ring_in, direct_in,
+    sel, gather, spread,
+    tok_sem, vec_sem, w_sem, mid_sem, send_sem, recv_sem, later_sem,
+    plane_send, plane_recv, ring_send, ring_recv, direct_send, direct_recv,
+    know_x, know_all, know_first, know_plane,
 ):
     ha, ta = lax.axis_index("ha"), lax.axis_index("ta")
     n_ha = lax.axis_size("ha")
@@ -32,6 +36,8 @@
         hx = (x + dx) % RING_X
         hz = (z + dz) % RING_Z
         return {"ha": hx * RING_Z + hz, "ta": 1 - ta if flip else ta}
+    ring_in[...] = jnp.zeros_like(ring_in)
+    direct_in[...] = jnp.zeros_like(direct_in)
     barrier = pltpu.get_barrier_semaphore()
 
     def greet(device):
@@ -118,17 +124,21 @@
 
         lax.fori_loop(0, channels // 16, rows, 0)
 
-    early = z < RING_Z // 2
+    early = z < 2
+    lower = z < RING_Z // 2
 
     @pl.when(early)
     def _():
         transform(0)
         transform(1)
     tok_copy.wait()
-    pairs = packed.shape[0]
-    for g in range(pairs):
-        packed[g] = jnp.concatenate([tok[2 * g].astype(F32), tok[2 * g + 1].astype(F32)], axis=-1).astype(BF16)
-    half = packed.shape[1]
+    lanes = tok.shape[2] // 2
+    for a in (0, 1):
+        for h in (0, 1):
+            packed[a, h] = jnp.concatenate(
+                [tok[4 * h + f, :, a * lanes : (a + 1) * lanes].astype(F32) for f in range(4)], axis=-1
+            ).astype(BF16)
+    half = packed.shape[2]
     own = pl.ds(ta * half, half)
     expected = (
         5
@@ -138,47 +148,57 @@
         + jnp.where(z == last, 1, 0)
     )
     pl.semaphore_wait(barrier, expected)
-    def tokens_to(to_ha, to_ta, place, slot):
-        if to_ta:
-            src, dst = packed, field.at[pl.ds(0, 4), place, own]
+    def tokens_copy(place, a, src_ta, to_ha, to_ta, slot, urgent):
+        there = pl.ds(src_ta * half, half)
+        frames = pl.ds(0, 2) if to_ta else pl.ds(1, 1)
+        of = pl.ds(0, 2) if to_ta else pl.ds(0, 1)
+        if a is None:
+            src, dst = packed.at[:, of], field.at[place, :, frames, there]
         else:
-            src, dst = packed.at[pl.ds(0, 2)], field.at[pl.ds(2, 2), place, own]
+            src, dst = packed.at[a, of], field.at[place, a, frames, there]
+        sem = recv_sem.at[place, src_ta] if urgent else later_sem.at[place // 2, src_ta]
         return pltpu.make_async_remote_copy(
-            src, dst, send_sem.at[slot], recv_sem.at[place, ta],
-            device_id={"ha": to_ha, "ta": to_ta}, device_id_type=MESH,
+            src, dst, send_sem.at[slot], sem, device_id={"ha": to_ha, "ta": to_ta}, device_id_type=MESH
         )
 
-    def tokens_from(place, src_ta, frames_8):
-        there = pl.ds(src_ta * half, half)
-        if frames_8:
-            src, dst = packed, field.at[pl.ds(0, 4), place, there]
-        else:
-            src, dst = packed.at[pl.ds(0, 2)], field.at[pl.ds(2, 2), place, there]
-        return pltpu.make_async_remote_copy(
-            src, dst, send_sem.at[0], recv_sem.at[place, src_ta],
-            device_id={"ha": ha, "ta": ta}, device_id_type=MESH,
-        )
-
-    def each_token_copy(act):
+    def each_token_copy(act, urgent):
         @pl.when(ha < n_ha - 1)
         def _():
-            act(tokens_to(ha + 1, 1, 0, 0))
-            act(tokens_to(ha + 1, 0, 0, 1))
+            for t in (1, 0):
+                act(tokens_copy(0, int(urgent), ta, ha + 1, t, 2 * (1 - int(urgent)) + t, urgent))
 
         @pl.when(ha > 0)
         def _():
-            act(tokens_to(ha - 1, 1, 2, 2))
-            act(tokens_to(ha - 1, 0, 2, 3))
-
-        @pl.when(ta == 0)
-        def _():
-            act(tokens_to(ha, 1, 1, 4))
-
-        @pl.when(ta == 1)
-        def _():
-            act(tokens_to(ha, 0, 1, 4))
-
-    each_token_copy(lambda copy: copy.start())
+            for t in (1, 0):
+                act(tokens_copy(2, 1 - int(urgent), ta, ha - 1, t, 4 + 2 * (1 - int(urgent)) + t, urgent))
+
+        if urgent:
+            for t in (1, 0):
+
+                @pl.when(ta == 1 - t)
+                def _():
+                    act(tokens_copy(1, None, ta, ha, t, 8, True))
+
+    def each_token_arrival(act, urgent):
+        for to_ta in (0, 1):
+
+            @pl.when(ta == to_ta)
+            def _():
+                if urgent:
+                    act(tokens_copy(1, None, 1 - to_ta, ha, to_ta, 8, True))
+
+                @pl.when(ha > 0)
+                def _():
+                    for t in (0, 1):
+                        act(tokens_copy(0, int(urgent), t, ha, to_ta, 0, urgent))
+
+                @pl.when(ha < n_ha - 1)
+                def _():
+                    for t in (0, 1):
+                        act(tokens_copy(2, 1 - int(urgent), t, ha, to_ta, 0, urgent))
+
+    each_token_copy(lambda copy: copy.start(), True)
+    each_token_copy(lambda copy: copy.start(), False)
 
     def tell(sem, device):
         pl.semaphore_signal(sem, inc=1, device_id=device, device_id_type=MESH)
@@ -187,15 +207,18 @@
     tell(know_x, near(RING_X - 1, 0, False))
 
     def pass_first(where, onwards):
-        @pl.when(where & (z >= 2))
+        @pl.when(where)
         def _():
             pl.semaphore_wait(know_first, 1)
 
-        @pl.when(where & (z >= 1) & onwards)
+        @pl.when(where & onwards)
         def _():
             tell(know_first, near(0, 1, False))
 
-    pass_first(early, True)
+    @pl.when(z == 1)
+    def _():
+        tell(know_first, near(0, 1, False))
+
     middle = (z == RING_Z // 2) | (z == RING_Z // 2 + 1)
 
     @pl.when(z == last)
@@ -204,20 +227,20 @@
             tell(know_all, near(0, d, False))
     @pl.when(ta == 0)
     def _():
-        field[0:2] = jnp.zeros_like(field[0:2])
-        field[2:4, 1, own] = packed[0:2]
+        field[:, :, 0] = jnp.zeros_like(field[:, :, 0])
+        field[1, :, 1, own] = packed[:, 0]
 
     @pl.when(ta == 1)
     def _():
-        field[0:4, 1, own] = packed[0:4]
+        field[1, :, :, own] = packed[...]
 
     @pl.when(ha == 0)
     def _():
-        field[:, 0] = jnp.zeros_like(field[:, 0])
+        field[0] = jnp.zeros_like(field[0])
 
     @pl.when(ha == n_ha - 1)
     def _():
-        field[:, 2] = jnp.zeros_like(field[:, 2])
+        field[2] = jnp.zeros_like(field[2])
 
     for high in (0, 1):
         w_big[high, :, 3 * (1 - high)] = jnp.zeros_like(w_big[high, :, 0])
@@ -225,52 +248,69 @@
             for q in range(3):
                 w_big[high, p, high + q, 48:64, :channels] = jnp.zeros((16, channels), BF16)
                 w_big[high, p, high + q, 0:16, channels:] = jnp.zeros((16, channels), BF16)
-    k = lax.broadcasted_iota(jnp.int32, sel.shape, 0)
-    n = lax.broadcasted_iota(jnp.int32, sel.shape, 1)
-    step, lane = k // 128, k % 128
-    column = 2 * step + (lane // 16) % 2 - 1
-    same = (lane // 32 == n // 64) & (lane % 16 == n % 16)
-    sel[...] = jnp.where(same & (column == (n // 16) % 4), 1.0, 0.0).astype(BF16)
-    k = lax.broadcasted_iota(jnp.int32, (channels, channels), 0)
-    n = lax.broadcasted_iota(jnp.int32, (channels, channels), 1)
-    member[...] = jnp.where(k // members == n // members, 1.0, 0.0).astype(BF16)
+    for i in range(16):
+        rest_ref[i, 3 * channels :, :rest] = jnp.zeros((channels, rest), BF16)
+        rest_ref[i, :channels, rest:] = jnp.zeros((channels, rest), BF16)
+    sel[...] = jnp.zeros_like(sel)
+    k = lax.broadcasted_iota(jnp.int32, (lanes, 128), 0)
+    n = lax.broadcasted_iota(jnp.int32, (lanes, 128), 1)
+    for a in (0, 1):
+        for step in range(3):
+            column = 2 * step + k // 16 - 1
+            block = (n // 64 == a) & (k % 16 == n % 16) & ((n // 16) % 4 == column)
+            block = jnp.where(block, 1.0, 0.0).astype(BF16)
+            for f in range(4):
+                sel[384 * a + 128 * step + lanes * f : 384 * a + 128 * step + lanes * (f + 1), 128 * f : 128 * f + 128] = block
+    k = lax.broadcasted_iota(jnp.int32, gather.shape, 0)
+    n = lax.broadcasted_iota(jnp.int32, gather.shape, 1)
+    gather[...] = jnp.where((k // members == n) & (n < 2 * GROUPS), 1.0, 0.0).astype(BF16)
+    k = lax.broadcasted_iota(jnp.int32, spread.shape, 0)
+    n = lax.broadcasted_iota(jnp.int32, spread.shape, 1)
+    spread[...] = jnp.where((n // members == k) & (k < 2 * GROUPS), 1.0, 0.0).astype(BF16)
     for copy in vector_copies:
         copy.wait()
+    stat_ref[2:3] = vectors[3].reshape(1, -1)
     for copy in w_copies:
         copy.wait()
-    for frames_8 in (False, True):
-
-        @pl.when(ta == int(frames_8))
-        def _():
-            tokens_from(1, int(not frames_8), frames_8).wait_recv()
-
-            @pl.when(ha > 0)
-            def _():
-                for t in (0, 1):
-                    tokens_from(0, t, frames_8).wait_recv()
-
-            @pl.when(ha < n_ha - 1)
-            def _():
-                for t in (0, 1):
-                    tokens_from(2, t, frames_8).wait_recv()
-    tokens = field.shape[2]
+    late = z >= RING_Z - LATE
+
+    def tell_plane(z0):
+        @pl.when(z == z0)
+        def _():
+            for to in range(RING_Z - LATE, RING_Z):
+                tell(know_plane.at[z0], {"ha": x * RING_Z + to, "ta": ta})
+
+    @pl.when(z <= 1)
+    def _():
+        pl.semaphore_wait(know_x, 2)
+        pl.semaphore_wait(know_all, 1)
+
+    tell_plane(0)
+    tell_plane(1)
+    pass_first((z == 2) | (z == 3), True)
+    each_token_arrival(lambda copy: copy.wait_recv(), True)
+    tokens = field.shape[3]
     row = lax.broadcasted_iota(jnp.int32, (tokens, 128), 0)
 
-    def patches(pairs_now):
-        for i in range(3):
-            stack = []
-            for g in pairs_now:
-                now = field[g, i].astype(F32)
-                left = jnp.where(row == 0, 0.0, pltpu.roll(now, 1, 0))
-                right = jnp.where(row == tokens - 1, 0.0, pltpu.roll(now, tokens - 1, 0))
-                stack.append(jnp.concatenate([left, now, right], axis=-1).astype(BF16))
-            moved = jnp.dot(jnp.concatenate(stack, axis=0), sel[...], preferred_element_type=F32)
-            moved = moved.astype(BF16)
-            for at, g in enumerate(pairs_now):
-                for f in (0, 1):
-                    patch[2 * g + f, i] = moved[at * tokens : (at + 1) * tokens, 128 * f : 128 * f + 128]
-
-    patches((1, 2, 3))
+    def patches(i, sides):
+        stack = []
+        for h in (0, 1):
+            pieces = []
+            for a in sides:
+                now = field[i, a, h].astype(F32)
+                pieces.append(jnp.where(row == 0, 0.0, pltpu.roll(now, 1, 0)))
+                pieces.append(now)
+                pieces.append(jnp.where(row == tokens - 1, 0.0, pltpu.roll(now, tokens - 1, 0)))
+            stack.append(jnp.concatenate(pieces, axis=-1).astype(BF16))
+        chosen = sel[384 * sides[0] : 384 * (sides[-1] + 1)]
+        moved = jnp.dot(jnp.concatenate(stack, axis=0), chosen, preferred_element_type=F32).astype(BF16)
+        for h in (0, 1):
+            for f in range(4):
+                patch[4 * h + f, i] = moved[h * tokens : (h + 1) * tokens, 128 * f : 128 * f + 128]
+
+    patches(0, (1,))
+    patches(1, (0, 1))
+    patches(2, (0,))
     bias = vectors[0].reshape(1, -1)
     bias = jnp.concatenate([bias, bias], axis=-1)
 
@@ -297,12 +337,36 @@
         values = hidden_rows(y, 2, 4)
         sums = sums + jnp.sum(values, axis=0, keepdims=True)
         squares = squares + jnp.sum(values * values, axis=0, keepdims=True)
-    for at, both in ((0, sums), (parts, squares)):
-        one = both[:, :channels] + both[:, channels:]
-        for part in range(parts):
-            mine[at + part : at + part + 1] = one[:, 128 * part : 128 * part + 128]
-    mine[2 * parts :] = jnp.zeros_like(mine[2 * parts :])
-    pl.semaphore_wait(know_x, 2)
+    def product(value, matrix):
+        terms = []
+        for _ in range(3):
+            term = value.astype(BF16)
+            terms.append(term.astype(F32))
+            value = value - terms[-1]
+        terms = jnp.concatenate(terms + [jnp.zeros((5, value.shape[1]), F32)], axis=0).astype(BF16)
+        result = jnp.dot(terms, matrix, preferred_element_type=F32)
+        return result[0:1] + result[1:2] + result[2:3]
+
+    folded = jnp.concatenate(
+        [both[:, :channels] + both[:, channels:] for both in (sums, squares)], axis=-1
+    )
+    mine[...] = product(folded, gather[...])
+    @pl.when(z > 1)
+    def _():
+        pl.semaphore_wait(know_x, 2)
+    def direct_to(z0, where):
+        @pl.when(late & where)
+        def _():
+            pl.semaphore_wait(know_plane.at[z0], 1)
+            for dx in (2, 1, 3, 0):
+                for flip in (1, 0):
+                    to = {"ha": (x + dx) % RING_X * RING_Z + z0, "ta": 1 - ta if flip else ta}
+                    pltpu.make_async_remote_copy(
+                        mine, direct_in.at[(last - z) * 8 + 2 * dx + flip], direct_send, direct_recv,
+                        device_id=to, device_id_type=MESH,
+                    ).start()
+
+    direct_to(0, z >= last - 1)
     plane = []
     for dx in (2, 1, 3, 0):
         for flip in (0, 1):
@@ -316,11 +380,18 @@
                 )
     for copy in plane:
         copy.start()
-    patches((0,))
+    direct_to(0, z < last - 1)
+    direct_to(1, True)
+    pass_first(lower & (z >= 4), True)
+    each_token_arrival(lambda copy: copy.wait_recv(), False)
+    patches(0, (0, 1))
+    patches(2, (0, 1))
     hidden_rows(0, 0, 6)
     hidden_rows(3, 0, 6)
     hidden_rows(1, 0, 2)
     hidden_rows(2, 0, 2)
+    for z0 in range(2, EARLY):
+        direct_to(z0, True)
     total = mine[...]
     all_plane = pltpu.make_async_remote_copy(
         plane_in, plane_in, plane_send, plane_recv, device_id=near(0, 0, True), device_id_type=MESH
@@ -335,66 +406,87 @@
             device_id=near(0, d, False), device_id_type=MESH,
         )
 
-    ring_copy(1).start()
-    for d in range(2, RING_Z):
-
-        @pl.when((z + d > RING_Z) | ((z == 1) & (d == last)))
+    def straight(d):
+        return late & (z + d >= RING_Z) & (z + d < RING_Z + EARLY)
+
+    for d in range(1, RING_Z):
+
+        @pl.when(jnp.logical_not(straight(d)) & ((d == 1) | (z + d > RING_Z) | ((z == 1) & (d == last))))
         def _():
             ring_copy(d).start()
 
     pass_first(middle, z == RING_Z // 2)
     for d in range(2, last):
 
-        @pl.when((early | middle) & (z + d == RING_Z))
+        @pl.when((lower | middle) & (z + d == RING_Z))
         def _():
             ring_copy(d).start()
-    for i in range(16):
-        rest_ref[i, 3 * channels :, :rest] = jnp.zeros((channels, rest), BF16)
-        rest_ref[i, :channels, rest:] = jnp.zeros((channels, rest), BF16)
-    stat_ref[2:3] = vectors[3].reshape(1, -1)
-
     @pl.when(early)
     def _():
         transform(2)
-    @pl.when(z < last)
+    @pl.when((z > 1) & (z < last))
     def _():
         pl.semaphore_wait(know_all, 1)
 
+    for z0 in range(2, EARLY):
+        tell_plane(z0)
     for d in range(2, RING_Z):
 
-        @pl.when((z + d <= last) | (jnp.logical_not(early | middle) & (z + d == RING_Z) & (z < last)))
+        @pl.when((z + d <= last) | (jnp.logical_not(lower | middle | late) & (z + d == RING_Z)))
         def _():
             ring_copy(d).start()
     @pl.when(jnp.logical_not(early))
     def _():
         for p in range(3):
             transform(p)
-    each_token_copy(lambda copy: copy.wait_send())
+    each_token_copy(lambda copy: copy.wait_send(), True)
+    each_token_copy(lambda copy: copy.wait_send(), False)
     all_plane.wait_send()
-    all_ring = pltpu.make_async_remote_copy(
-        ring_in, ring_in, ring_send, ring_recv, device_id=near(0, 1, False), device_id_type=MESH
-    )
-    all_ring.wait_recv()
+    def ring_copies(number):
+        return pltpu.make_async_remote_copy(
+            ring_in.at[pl.ds(0, number)], ring_in.at[pl.ds(0, number)], ring_send, ring_recv,
+            device_id=near(0, 1, False), device_id_type=MESH,
+        )
+
+    def direct_copies(number):
+        return pltpu.make_async_remote_copy(
+            direct_in.at[pl.ds(0, number)], direct_in.at[pl.ds(0, number)], direct_send, direct_recv,
+            device_id=near(0, 1, False), device_id_type=MESH,
+        )
+
+    @pl.when(z < EARLY)
+    def _():
+        ring_copies(last - LATE).wait_recv()
+    @pl.when(z < EARLY)
+    def _():
+        direct_copies(8 * LATE).wait_recv()
+
+    @pl.when(z >= EARLY)
+    def _():
+        ring_copies(last).wait_recv()
+
     for slot in range(ring_in.shape[0]):
         total = total + ring_in[slot]
+    rows = [direct_in[slot] for slot in range(8 * LATE)]
+    while len(rows) > 1:
+        rows = [sum(rows[at + 1 : at + 2], rows[at]) for at in range(0, len(rows), 2)]
+    total = total + rows[0]
     count = n_ha * lax.axis_size("ta") * 4 * 2 * 2 * tokens * members
-    sums = jnp.concatenate([total[part : part + 1] for part in range(parts)], axis=-1)
-    squares = jnp.concatenate([total[parts + part : parts + part + 1] for part in range(parts)], axis=-1)
-    terms = []
-    for value in (sums, squares):
-        for _ in range(3):
-            term = value.astype(BF16)
-            terms.append(term.astype(F32))
-            value = value - terms[-1]
-    terms = jnp.concatenate(terms + [jnp.zeros((2, channels), F32)], axis=0).astype(BF16)
-    shared = jnp.dot(terms, member[...], preferred_element_type=F32) * (1.0 / count)
-    mean = shared[0:1] + shared[1:2] + shared[2:3]
-    square = shared[3:4] + shared[4:5] + shared[5:6]
+    shared = product(total * (1.0 / count), spread[...])
+    mean, square = shared[:, :channels], shared[:, channels:]
     var = jnp.maximum(square - mean * mean, 0.0)
     scale = lax.rsqrt(var + EPS) * vectors[1].reshape(1, -1)
     stat_ref[0:1] = 0.5 * scale
     stat_ref[1:2] = 0.5 * (vectors[2].reshape(1, -1) - mean * scale)
-    all_ring.wait_send()
+
+    @pl.when(late)
+    def _():
+        ring_copies(last - EARLY).wait_send()
+        direct_copies(8 * EARLY).wait_send()
+
+    @pl.when(jnp.logical_not(late))
+    def _():
+        ring_copies(last).wait_send()
 
 
 def decode_kernel(
@@ -409,39 +501,44 @@
     frames, rows = frames_in - 2, rows_in - 2
     wide = main_ref.shape[2]
     rest = channels - wide
-    for part in range(parts):
+    for slot in (0, 1):
+        for part in range(parts):
+            for y in range(rows_in):
+                shifted[slot, part, y, 0, 8 + tokens :] = jnp.zeros((8, 128), F32)
+                shifted[slot, part, y, 1, :8] = jnp.zeros((8, 128), F32)
+
+    def activate(f):
         for y in range(rows_in):
-            shifted[part, y, 0, 8 + tokens :] = jnp.zeros((8, 128), F32)
-            shifted[part, y, 1, :8] = jnp.zeros((8, 128), F32)
-
-    def activate(f, carry):
-        inside = [
-            (f >= 2 - 2 * ta) & (ha * rows + y >= 1) & (ha * rows + y <= n_ha * rows) for y in range(rows_in)
-        ]
+            inside = (ha * rows + y >= 1) & (ha * rows + y <= n_ha * rows)
+            if f < 2:
+                inside = inside & (ta > 0)
+            for part in range(parts):
+                lanes = slice(128 * part, 128 * part + 128)
+                row_scale = jnp.where(inside, stat_ref[0:1, lanes], 0.0)
+                row_shift = jnp.where(inside, stat_ref[1:2, lanes], 0.0)
+                for b in (0, 1):
+                    value = h_ref[f, y, b * parts + part] * row_scale + row_shift
+                    shifted[f % 2, part, y, b, 8 : 8 + tokens] = value + value * jnp.tanh(value)
+
+    def by_columns(f):
         for y in range(rows_in):
             by_part = []
             for part in range(parts):
-                lanes = slice(128 * part, 128 * part + 128)
-                row_scale = jnp.where(inside[y], stat_ref[0:1, lanes], 0.0)
-                row_shift = jnp.where(inside[y], stat_ref[1:2, lanes], 0.0)
-                columns = []
-                for b in (0, 1):
-                    value = h_ref[f, y, b * parts + part] * row_scale + row_shift
-                    value = value + value * jnp.tanh(value)
-                    shifted[part, y, b, 8 : 8 + tokens] = value
-                    columns.append(value)
-                even, odd = columns
-                before = shifted[part, y, 1, 7 : 7 + tokens]
-                after = shifted[part, y, 0, 9 : 9 + tokens]
+                even, odd = [shifted[f % 2, part, y, b, 8 : 8 + tokens] for b in (0, 1)]
+                before = shifted[f % 2, part, y, 1, 7 : 7 + tokens]
+                after = shifted[f % 2, part, y, 0, 9 : 9 + tokens]
                 by_part.append((before - odd, even + odd, odd - even, even - after))
             for k in range(4):
                 value = jnp.concatenate([by_part[part][k] for part in range(wide // 128)], axis=-1)
                 columns_wide[k, f, y] = value.astype(BF16)
                 value = jnp.concatenate([by_part[part][k] for part in range(wide // 128, parts)], axis=-1)
                 columns_rest[k, f, y] = value.astype(BF16)
-        return carry
-
-    lax.fori_loop(0, frames_in, activate, 0)
+
+    activate(0)
+    for f in range(frames_in):
+        if f + 1 < frames_in:
+            activate(f + 1)
+        by_columns(f)
 
     def by_rows(i, k):
         one, two = ((0, 2), (1, 2), (2, 1), (1, 3))[i]
@@ -540,23 +637,28 @@
         scratch_shapes=[
             pltpu.VMEM(latent_tokens.shape, BF16),
             pltpu.VMEM((4, channels), F32),
-            pltpu.VMEM((4, half, 128), BF16),
-            pltpu.VMEM((4, 3, tokens, 128), BF16),
+            pltpu.VMEM((2, 2, half, 128), BF16),
+            pltpu.VMEM((3, 2, 2, tokens, 128), BF16),
             pltpu.VMEM((8, 3, tokens, 128), BF16),
             pltpu.VMEM((2, 3, 4, 64, 2 * channels), BF16),
             pltpu.VMEM(w_mid.shape, BF16),
-            pltpu.VMEM((8, 128), F32),
-            pltpu.VMEM((7, 8, 128), F32),
-            pltpu.VMEM((8, 128), F32),
-            pltpu.VMEM((RING_Z - 1, 8, 128), F32),
-            pltpu.VMEM((384, 256), BF16),
-            pltpu.VMEM((channels, channels), BF16),
+            pltpu.VMEM((1, 128), F32),
+            pltpu.VMEM((7, 1, 128), F32),
+            pltpu.VMEM((1, 128), F32),
+            pltpu.VMEM((RING_Z - 1, 1, 128), F32),
+            pltpu.VMEM((8 * max(LATE, EARLY), 1, 128), F32),
+            pltpu.VMEM((2 * 384, 4 * 128), BF16),
+            pltpu.VMEM((2 * channels, 128), BF16),
+            pltpu.VMEM((128, 2 * channels), BF16),
             pltpu.SemaphoreType.DMA,
             pltpu.SemaphoreType.DMA((4,)),
             pltpu.SemaphoreType.DMA((4,)),
             pltpu.SemaphoreType.DMA((3,)),
-            pltpu.SemaphoreType.DMA((5,)),
+            pltpu.SemaphoreType.DMA((9,)),
             pltpu.SemaphoreType.DMA((3, 2)),
+            pltpu.SemaphoreType.DMA((2, 2)),
+            pltpu.SemaphoreType.DMA,
+            pltpu.SemaphoreType.DMA,
             pltpu.SemaphoreType.DMA,
             pltpu.SemaphoreType.DMA,
             pltpu.SemaphoreType.DMA,
@@ -564,6 +666,7 @@
             pltpu.SemaphoreType.REGULAR,
             pltpu.SemaphoreType.REGULAR,
             pltpu.SemaphoreType.REGULAR,
+            pltpu.SemaphoreType.REGULAR((EARLY,)),
         ],
         compiler_params=pltpu.CompilerParams(
             collective_id=0, has_side_effects=True, vmem_limit_bytes=20 * 2**20
@@ -576,7 +679,7 @@
         in_specs=[vmem, vmem, vmem, vmem],
         out_specs=hbm,
         scratch_shapes=[
-            pltpu.VMEM((parts, 4, 2, tokens + 16, 128), F32),
+            pltpu.VMEM((2, parts, 4, 2, tokens + 16, 128), F32),
             pltpu.VMEM((4, 6, 4, tokens, wide), BF16),
             pltpu.VMEM((4, 6, 4, tokens, rest), BF16),
             pltpu.VMEM((2, 6, tokens, wide), BF16),
@@ -586,7 +689,7 @@
             pltpu.VMEM((4, 2, 2 * tokens, channels), BF16),
             pltpu.SemaphoreType.DMA((8,)),
         ],
-        compiler_params=pltpu.CompilerParams(vmem_limit_bytes=18 * 2**20),
+        compiler_params=pltpu.CompilerParams(vmem_limit_bytes=20 * 2**20),
         name="decode",
     )(*prepared)
 

time: 46.2 us -> 44.1 us (0.955)
  Pallas kernels: 46.1 us -> 43.8 us
    pallas_call x1, Pallas kernels: 37.9 us -> 36.2 us  [body(): pl.pallas_call(exchange_kernel, out_shape=(jax.ShapeDtypeStruct((6, 4, 2...]
    pallas_call x1, Pallas kernels: 8.23 us -> 7.54 us  [body(): pl.pallas_call(decode_kernel, out_shape=jax.ShapeDtypeStruct((4, 2, 2 * t...]
where the time goes in v3:
time: 44.1 us; the launch traced here: 44 us
  Pallas kernels  43.8 us (99%)
    pallas_call x1, Pallas kernels, body(): pl.pallas_call(exchange_kernel, out_shape=(jax.ShapeDtypeStruct((6, 4, 2...  36.2 us
    pallas_call x1, Pallas kernels, body(): pl.pallas_call(decode_kernel, out_shape=jax.ShapeDtypeStruct((4, 2, 2 * t...  7.54 us

profile of v3, /device:TPU:33, one launch (start us, length us, event | category | flops | bytes accessed | tf_op | source)
XLA Modules:
  0.0 44.0 jit_solution(4234528420570499716)
XLA Ops:
  0.0 36.2 %exchange.1 = (f32[6,4,6,64,128]{4,3,2,1,0:T(8,128)S(1)}, f32[3,384]{1,0:T(4,128)S(1)}, bf16[16,1152,256]{2,1,0:T(8,128)(2,1)S(1)}, bf16[16,1536,256]{2,1,0:T(8,128)(2,1)S(1)}) custom-call(bf16[8,32,64]{2,1,0:T(8,128)(2,1)} %tok_hbm.1, bf16[3,3,48,384]{3,2,1,0:T(8,128)(2,1)} %bitcast.1, f32[384]{0:T(512)} %b_hbm.1, f32[384]{0:T(512)} %gain_hbm.1, ...), custom_call_target="tpu_custom_call" | custom-call | tf_op jit(solution)/shard_map/exchange/pallas_call | solution.py:627
  36.3 7.5 %decode.1 = bf16[4,2,128,384]{3,2,1,0:T(8,128)(2,1)} custom-call(f32[6,4,6,64,128]{4,3,2,1,0:T(8,128)S(1)} %get-tuple-element.9.h_ref, f32[3,384]{1,0:T(4,128)S(1)} %get-tuple-element.10.stat_ref, bf16[16,1152,256]{2,1,0:T(8,128)(2,1)S(1)} %get-tuple-element.11.main_ref, bf16[16,1536,256]{2,1,0:T(8,128)(2,1)S(1)} %get-tuple-element.12.rest_ref), custom_call_target="tpu_custom_call" | custom-call | tf_op jit(solution)/shard_map/decode/pallas_call | solution.py:676

commit v4 on v3

--- a/solution.py
+++ b/solution.py
@@ -19,7 +19,7 @@
 def exchange_kernel(
     tok_hbm, w_hbm, b_hbm, gain_hbm, shift_hbm, b_mid_hbm, mid_hbm,
     h_ref, stat_ref, main_ref, rest_ref,
-    tok, vectors, packed, field, patch, w_big, mid, mine, plane_in, plane_sum, ring_in, direct_in,
+    tok, vectors, packed, field, patch, partial, w_big, mid, mine, plane_in, plane_sum, ring_in, direct_in,
     sel, gather, spread,
     tok_sem, vec_sem, w_sem, mid_sem, send_sem, recv_sem, later_sem,
     plane_send, plane_recv, ring_send, ring_recv, direct_send, direct_recv,
@@ -130,6 +130,11 @@
     @pl.when(early)
     def _():
         transform(0)
+
+    first = (ha == 0) & (ta == 0)
+
+    @pl.when(early & jnp.logical_not(first))
+    def _():
         transform(1)
     tok_copy.wait()
     lanes = tok.shape[2] // 2
@@ -184,8 +189,9 @@
 
             @pl.when(ta == to_ta)
             def _():
-                if urgent:
+                if urgent is None:
                     act(tokens_copy(1, None, 1 - to_ta, ha, to_ta, 8, True))
+                    return
 
                 @pl.when(ha > 0)
                 def _():
@@ -197,12 +203,16 @@
                     for t in (0, 1):
                         act(tokens_copy(2, 1 - int(urgent), t, ha, to_ta, 0, urgent))
 
-    each_token_copy(lambda copy: copy.start(), True)
-    each_token_copy(lambda copy: copy.start(), False)
-
     def tell(sem, device):
         pl.semaphore_signal(sem, inc=1, device_id=device, device_id_type=MESH)
 
+    @pl.when(z == last)
+    def _():
+        for d in range(1, 1 + EARLY):
+            tell(know_all, near(0, d, False))
+
+    each_token_copy(lambda copy: copy.start(), True)
+
     tell(know_x, near(1, 0, False))
     tell(know_x, near(RING_X - 1, 0, False))
 
@@ -223,7 +233,7 @@
 
     @pl.when(z == last)
     def _():
-        for d in range(1, RING_Z):
+        for d in range(1 + EARLY, RING_Z):
             tell(know_all, near(0, d, False))
     @pl.when(ta == 0)
     def _():
@@ -272,6 +282,11 @@
     stat_ref[2:3] = vectors[3].reshape(1, -1)
     for copy in w_copies:
         copy.wait()
+    each_token_copy(lambda copy: copy.start(), False)
+
+    @pl.when(first)
+    def _():
+        transform(1)
     late = z >= RING_Z - LATE
 
     def tell_plane(z0):
@@ -288,7 +303,7 @@
     tell_plane(0)
     tell_plane(1)
     pass_first((z == 2) | (z == 3), True)
-    each_token_arrival(lambda copy: copy.wait_recv(), True)
+    each_token_arrival(lambda copy: copy.wait_recv(), None)
     tokens = field.shape[3]
     row = lax.broadcasted_iota(jnp.int32, (tokens, 128), 0)
 
@@ -308,11 +323,13 @@
             for f in range(4):
                 patch[4 * h + f, i] = moved[h * tokens : (h + 1) * tokens, 128 * f : 128 * f + 128]
 
-    patches(0, (1,))
-    patches(1, (0, 1))
-    patches(2, (0,))
     bias = vectors[0].reshape(1, -1)
     bias = jnp.concatenate([bias, bias], axis=-1)
+
+    def keep_hidden(y, first, frames, total):
+        for n in range(2 * parts):
+            part = total[:, 128 * n : 128 * n + 128].astype(BF16).astype(F32)
+            h_ref[first : first + frames, y, n] = part.reshape(frames, tokens, 128)
 
     def hidden_rows(y, first, frames):
         low, high = y // 2, y % 2
@@ -325,16 +342,33 @@
             total = total + jnp.dot(
                 lhs, w_big[high, p].reshape(256, 2 * channels), preferred_element_type=F32
             )
-        total = total.astype(BF16).astype(F32)
-        for n in range(2 * parts):
-            part = total[:, 128 * n : 128 * n + 128]
-            h_ref[first : first + frames, y, n] = part.reshape(frames, tokens, 128)
-        return total
-
+        keep_hidden(y, first, frames, total)
+
+    def part_of_own(y, i, start):
+        low, high = y // 2, y % 2
+        taps = [
+            (
+                patch[2 + p : 6 + p, i].reshape(4 * tokens, 128),
+                w_big[high, p, 2 * (i - low) : 2 * (i - low) + 2].reshape(128, 2 * channels),
+            )
+            for p in range(3)
+        ]
+        lhs = jnp.concatenate([taps[0][0], taps[1][0]], axis=-1)
+        rhs = jnp.concatenate([taps[0][1], taps[1][1]], axis=0)
+        total = start + jnp.dot(lhs, rhs, preferred_element_type=F32)
+        return total + jnp.dot(*taps[2], preferred_element_type=F32)
+
+    patches(1, (0, 1))
+    for y in (1, 2):
+        partial[y - 1] = part_of_own(y, 1, bias)
+    each_token_arrival(lambda copy: copy.wait_recv(), True)
+    patches(0, (1,))
+    patches(2, (0,))
     sums = jnp.zeros((1, 2 * channels), F32)
     squares = jnp.zeros((1, 2 * channels), F32)
     for y in (1, 2):
-        values = hidden_rows(y, 2, 4)
+        values = part_of_own(y, 2 * (y - 1), partial[y - 1])
+        keep_hidden(y, 2, 4, values)
         sums = sums + jnp.sum(values, axis=0, keepdims=True)
         squares = squares + jnp.sum(values * values, axis=0, keepdims=True)
     def product(value, matrix):
@@ -387,10 +421,11 @@
     patches(0, (0, 1))
     patches(2, (0, 1))
     hidden_rows(0, 0, 6)
+    direct_to(2, True)
     hidden_rows(3, 0, 6)
     hidden_rows(1, 0, 2)
     hidden_rows(2, 0, 2)
-    for z0 in range(2, EARLY):
+    for z0 in range(3, EARLY):
         direct_to(z0, True)
     total = mine[...]
     all_plane = pltpu.make_async_remote_copy(
@@ -409,22 +444,22 @@
     def straight(d):
         return late & (z + d >= RING_Z) & (z + d < RING_Z + EARLY)
 
-    for d in range(1, RING_Z):
-
-        @pl.when(jnp.logical_not(straight(d)) & ((d == 1) | (z + d > RING_Z) | ((z == 1) & (d == last))))
-        def _():
-            ring_copy(d).start()
-
     pass_first(middle, z == RING_Z // 2)
-    for d in range(2, last):
-
-        @pl.when((lower | middle) & (z + d == RING_Z))
+    upper = (z > RING_Z // 2 + 1) & jnp.logical_not(late)
+
+    @pl.when(upper)
+    def _():
+        pl.semaphore_wait(know_all, 1)
+
+    for d in (*range(5, RING_Z), *range(1, 5)):
+
+        @pl.when(jnp.logical_not(straight(d)) & ((d == 1) | (z + d >= RING_Z)))
         def _():
             ring_copy(d).start()
     @pl.when(early)
     def _():
         transform(2)
-    @pl.when((z > 1) & (z < last))
+    @pl.when((z > 1) & (z < last) & jnp.logical_not(upper))
     def _():
         pl.semaphore_wait(know_all, 1)
 
@@ -432,7 +467,7 @@
         tell_plane(z0)
     for d in range(2, RING_Z):
 
-        @pl.when((z + d <= last) | (jnp.logical_not(lower | middle | late) & (z + d == RING_Z)))
+        @pl.when(z + d <= last)
         def _():
             ring_copy(d).start()
     @pl.when(jnp.logical_not(early))
@@ -491,7 +526,7 @@
 
 def decode_kernel(
     h_ref, stat_ref, main_ref, rest_ref, out_hbm,
-    shifted, columns_wide, columns_rest, planes_wide, planes_rest, acc, rows_f32, out, out_sem,
+    shifted, columns_wide, columns_rest, planes_wide, planes_rest, products, total, rows_f32, out, out_sem,
 ):
     ha, ta = lax.axis_index("ha"), lax.axis_index("ta")
     n_ha = lax.axis_size("ha")
@@ -501,44 +536,43 @@
     frames, rows = frames_in - 2, rows_in - 2
     wide = main_ref.shape[2]
     rest = channels - wide
-    for slot in (0, 1):
+    for f in range(frames_in):
         for part in range(parts):
             for y in range(rows_in):
-                shifted[slot, part, y, 0, 8 + tokens :] = jnp.zeros((8, 128), F32)
-                shifted[slot, part, y, 1, :8] = jnp.zeros((8, 128), F32)
-
-    def activate(f):
-        for y in range(rows_in):
+                shifted[f, part, y, 0, 8 + tokens :] = jnp.zeros((8, 128), F32)
+                shifted[f, part, y, 1, :8] = jnp.zeros((8, 128), F32)
+
+    held = {}
+
+    def activate(y, b):
+        later = held.get("product", 0.0)
+        for f in range(frames_in):
             inside = (ha * rows + y >= 1) & (ha * rows + y <= n_ha * rows)
             if f < 2:
                 inside = inside & (ta > 0)
             for part in range(parts):
                 lanes = slice(128 * part, 128 * part + 128)
-                row_scale = jnp.where(inside, stat_ref[0:1, lanes], 0.0)
+                row_scale = jnp.where(inside, stat_ref[0:1, lanes], 0.0) + later
                 row_shift = jnp.where(inside, stat_ref[1:2, lanes], 0.0)
-                for b in (0, 1):
-                    value = h_ref[f, y, b * parts + part] * row_scale + row_shift
-                    shifted[f % 2, part, y, b, 8 : 8 + tokens] = value + value * jnp.tanh(value)
-
-    def by_columns(f):
-        for y in range(rows_in):
-            by_part = []
-            for part in range(parts):
-                even, odd = [shifted[f % 2, part, y, b, 8 : 8 + tokens] for b in (0, 1)]
-                before = shifted[f % 2, part, y, 1, 7 : 7 + tokens]
-                after = shifted[f % 2, part, y, 0, 9 : 9 + tokens]
-                by_part.append((before - odd, even + odd, odd - even, even - after))
-            for k in range(4):
-                value = jnp.concatenate([by_part[part][k] for part in range(wide // 128)], axis=-1)
-                columns_wide[k, f, y] = value.astype(BF16)
-                value = jnp.concatenate([by_part[part][k] for part in range(wide // 128, parts)], axis=-1)
-                columns_rest[k, f, y] = value.astype(BF16)
-
-    activate(0)
-    for f in range(frames_in):
-        if f + 1 < frames_in:
-            activate(f + 1)
-        by_columns(f)
+                value = h_ref[f, y, b * parts + part] * row_scale + row_shift
+                shifted[f, part, y, b, 8 : 8 + tokens] = value + value * jnp.tanh(value)
+
+    def by_columns(y, k):
+        def one(f, part):
+            even, odd = [shifted.at[f, part, y, b] for b in (0, 1)]
+            if k == 0:
+                return odd[7 : 7 + tokens] - odd[8 : 8 + tokens]
+            if k == 1:
+                return even[8 : 8 + tokens] + odd[8 : 8 + tokens]
+            if k == 2:
+                return odd[8 : 8 + tokens] - even[8 : 8 + tokens]
+            return even[8 : 8 + tokens] - even[9 : 9 + tokens]
+
+        for f in range(frames_in):
+            value = jnp.concatenate([one(f, part) for part in range(wide // 128)], axis=-1)
+            columns_wide[k, f, y] = value.astype(BF16)
+            value = jnp.concatenate([one(f, part) for part in range(wide // 128, parts)], axis=-1)
+            columns_rest[k, f, y] = value.astype(BF16)
 
     def by_rows(i, k):
         one, two = ((0, 2), (1, 2), (2, 1), (1, 3))[i]
@@ -548,66 +582,96 @@
             else:
                 planes[k % 2] = columns[k, :, one] - columns[k, :, two]
 
+    ahead = {
+        0: [(activate, 0, 0), (activate, 2, 0), (by_columns, 0, 1), (by_columns, 2, 1)],
+        1: [(by_columns, 0, 2), (by_columns, 2, 2), (activate, 1, 1)],
+        2: [(by_columns, 0, 3), (by_columns, 2, 3), (activate, 1, 0)],
+        3: [(by_columns, 1, 0), (by_columns, 1, 1)],
+        4: [(by_columns, 1, 2), (by_columns, 1, 3)],
+        5: [(activate, 3, 1)],
+        6: [(activate, 3, 0)],
+        7: [(by_columns, 3, 0)],
+        8: [(by_columns, 3, 1)],
+        9: [(by_columns, 3, 2)],
+        10: [(by_columns, 3, 3)],
+    }
+    for y in (0, 2):
+        activate(y, 1)
+    for y in (0, 2):
+        by_columns(y, 0)
     by_rows(0, 0)
     bias = stat_ref[2:3]
     copies = []
 
-    def finish(y):
-        for f in range(frames):
-            for part in range(parts):
-                lanes = slice(128 * part, 128 * part + 128)
-                for b in (0, 1):
-                    hidden = h_ref[f + 2, y + 1, b * parts + part]
-                    rows_f32[y, f, part, pl.ds(b, tokens, stride=2)] = acc[y, b, f, part] + (
-                        hidden + bias[:, lanes]
-                    )
-                out[f, y, :, lanes] = rows_f32[y, f, part].astype(BF16)
-            copies.append(pltpu.make_async_copy(out.at[f, y], out_hbm.at[f, y], out_sem.at[frames * y + f]))
-            copies[-1].start()
-
-    signs = ((1, 1, 1, 0), (0, 1, -1, -1))
-    first = [[True, True], [True, True]]
+    def done(y, b, f, part, value):
+        hidden = h_ref[f + 2, y + 1, b * parts + part] + bias[:, 128 * part : 128 * part + 128]
+        rows_f32[y, f, part, pl.ds(b, tokens, stride=2)] = value + hidden
+
+    def send(y, f):
+        for part in range(parts):
+            out[f, y, :, 128 * part : 128 * part + 128] = rows_f32[y, f, part].astype(BF16)
+        copies.append(pltpu.make_async_copy(out.at[f, y], out_hbm.at[f, y], out_sem.at[frames * y + f]))
+        copies[-1].start()
+
+    def combine(i, f):
+        for part in range(parts):
+            m0, m1, m2, m3 = [products[i % 2, k, f, part] for k in range(4)]
+            for b, value in ((0, m0 + m1 + m2), (1, m1 - m2 - m3)):
+                if i == 0:
+                    total[0, b, f, part] = value
+                elif i == 1:
+                    total[0, b, f, part] = total[0, b, f, part] + value
+                    total[1, b, f, part] = value
+                elif i == 2:
+                    done(0, b, f, part, total[0, b, f, part] + value)
+                    total[1, b, f, part] = total[1, b, f, part] - value
+        if i == 2:
+            send(0, f)
+
+    def last_even(f):
+        for part in range(parts):
+            m0, m1, m2 = [products[1, k, f, part] for k in range(3)]
+            done(1, 0, f, part, total[1, 0, f, part] - (m0 + m1 + m2))
+            total[1, 1, f, part] = total[1, 1, f, part] - (m1 - m2)
+
+    def last_odd(f):
+        for part in range(parts):
+            done(1, 1, f, part, total[1, 1, f, part] + products[1, 3, f, part])
+        send(1, f)
+
     for i in range(4):
         for k in range(4):
             at = 4 * i + k
+            for make, one, two in ahead.get(at, ()):
+                make(one, two)
             if at < 15:
                 by_rows((at + 1) // 4, (at + 1) % 4)
+            if i and k < 2:
+                combine(i - 1, 2 * k)
+                combine(i - 1, 2 * k + 1)
+            if at == 15:
+                for f in range(frames):
+                    last_even(f)
             both = (planes_wide.at[k % 2], planes_rest.at[k % 2])
             lhs = [planes[p : p + frames] for p in range(3) for planes in both]
             lhs = jnp.concatenate(lhs, axis=-1).reshape(frames * tokens, 3 * channels)
             product = jnp.dot(lhs, main_ref[at], preferred_element_type=F32)
+            held["product"] = 0.0 * product[0:1, 0:128]
+            for part in range(wide // 128):
+                products[i % 2, k, :, part] = product[:, 128 * part : 128 * part + 128].reshape(frames, tokens, 128)
             lhs = [
                 jnp.concatenate([planes[t + p] for p in range(4) for planes in both], axis=-1)
                 for t in range(0, frames, 2)
             ]
-            other = jnp.dot(jnp.concatenate(lhs, axis=0), rest_ref[at], preferred_element_type=F32)
-            for y in (0, 1):
-                for b in (0, 1):
-                    sign = signs[y][i] * signs[b][k]
-                    if not sign:
-                        continue
-                    for f in range(frames):
-                        for part in range(parts):
-                            if 128 * part < wide:
-                                value = product[f * tokens : (f + 1) * tokens, 128 * part : 128 * part + 128]
-                            else:
-                                value = other[
-                                    f // 2 * tokens : (f // 2 + 1) * tokens,
-                                    rest * (f % 2) : rest * (f % 2) + rest,
-                                ]
-                            if first[y][b]:
-                                acc[y, b, f, part] = value if sign > 0 else -value
-                            elif sign > 0:
-                                acc[y, b, f, part] = acc[y, b, f, part] + value
-                            else:
-                                acc[y, b, f, part] = acc[y, b, f, part] - value
-                    first[y][b] = False
-        if i == 2:
-            finish(0)
-    finish(1)
-    for y in (0, 1):
-        for f in range(frames):
-            copies[frames * y + f].wait()
+            product = jnp.dot(jnp.concatenate(lhs, axis=0), rest_ref[at], preferred_element_type=F32)
+            for f in range(frames):
+                products[i % 2, k, f, wide // 128] = product[
+                    f // 2 * tokens : (f // 2 + 1) * tokens, rest * (f % 2) : rest * (f % 2) + rest
+                ]
+    for f in range(frames):
+        last_odd(f)
+    for copy in copies:
+        copy.wait()
 
 
 def keep(value):
@@ -640,6 +704,7 @@
             pltpu.VMEM((2, 2, half, 128), BF16),
             pltpu.VMEM((3, 2, 2, tokens, 128), BF16),
             pltpu.VMEM((8, 3, tokens, 128), BF16),
+            pltpu.VMEM((2, 4 * tokens, 2 * channels), F32),
             pltpu.VMEM((2, 3, 4, 64, 2 * channels), BF16),
             pltpu.VMEM(w_mid.shape, BF16),
             pltpu.VMEM((1, 128), F32),
@@ -679,17 +744,18 @@
         in_specs=[vmem, vmem, vmem, vmem],
         out_specs=hbm,
         scratch_shapes=[
-            pltpu.VMEM((2, parts, 4, 2, tokens + 16, 128), F32),
+            pltpu.VMEM((6, parts, 4, 2, tokens + 16, 128), F32),
             pltpu.VMEM((4, 6, 4, tokens, wide), BF16),
             pltpu.VMEM((4, 6, 4, tokens, rest), BF16),
             pltpu.VMEM((2, 6, tokens, wide), BF16),
             pltpu.VMEM((2, 6, tokens, rest), BF16),
+            pltpu.VMEM((2, 4, 4, parts, tokens, 128), F32),
             pltpu.VMEM((2, 2, 4, parts, tokens, 128), F32),
             pltpu.VMEM((2, 4, parts, 2 * tokens, 128), F32),
             pltpu.VMEM((4, 2, 2 * tokens, channels), BF16),
             pltpu.SemaphoreType.DMA((8,)),
         ],
-        compiler_params=pltpu.CompilerParams(vmem_limit_bytes=20 * 2**20),
+        compiler_params=pltpu.CompilerParams(vmem_limit_bytes=28 * 2**20),
         name="decode",
     )(*prepared)
 

time: 44.1 us -> 43 us (0.975)
  Pallas kernels: 43.8 us -> 42.7 us
    pallas_call x1, Pallas kernels: 36.2 us -> 35.4 us  [body(): pl.pallas_call(exchange_kernel, out_shape=(jax.ShapeDtypeStruct((6, 4, 2...]
where the time goes in v4:
time: 43 us; the launch traced here: 42.8 us
  Pallas kernels  42.7 us (99%)
    pallas_call x1, Pallas kernels, body(): pl.pallas_call(exchange_kernel, out_shape=(jax.ShapeDtypeStruct((6, 4, 2...  35.4 us
    pallas_call x1, Pallas kernels, body(): pl.pallas_call(decode_kernel, out_shape=jax.ShapeDtypeStruct((4, 2, 2 * t...  7.27 us

profile of v4, /device:TPU:33, one launch (start us, length us, event | category | flops | bytes accessed | tf_op | source)
XLA Modules:
  0.0 42.8 jit_solution(5878795666663279704)
XLA Ops:
  0.0 35.4 %exchange.1 = (f32[6,4,6,64,128]{4,3,2,1,0:T(8,128)S(1)}, f32[3,384]{1,0:T(4,128)S(1)}, bf16[16,1152,256]{2,1,0:T(8,128)(2,1)S(1)}, bf16[16,1536,256]{2,1,0:T(8,128)(2,1)S(1)}) custom-call(bf16[8,32,64]{2,1,0:T(8,128)(2,1)} %tok_hbm.1, bf16[3,3,48,384]{3,2,1,0:T(8,128)(2,1)} %bitcast.1, f32[384]{0:T(512)} %b_hbm.1, f32[384]{0:T(512)} %gain_hbm.1, ...), custom_call_target="tpu_custom_call" | custom-call | tf_op jit(solution)/shard_map/exchange/pallas_call | solution.py:691
  35.4 7.3 %decode.1 = bf16[4,2,128,384]{3,2,1,0:T(8,128)(2,1)} custom-call(f32[6,4,6,64,128]{4,3,2,1,0:T(8,128)S(1)} %get-tuple-element.9.h_ref, f32[3,384]{1,0:T(4,128)S(1)} %get-tuple-element.10.stat_ref, bf16[16,1152,256]{2,1,0:T(8,128)(2,1)S(1)} %get-tuple-element.11.main_ref, bf16[16,1536,256]{2,1,0:T(8,128)(2,1)S(1)} %get-tuple-element.12.rest_ref), custom_call_target="tpu_custom_call" | custom-call | tf_op jit(solution)/shard_map/decode/pallas_call | solution.py:741

commit v5 on v4

--- a/solution.py
+++ b/solution.py
@@ -21,7 +21,7 @@
     h_ref, stat_ref, main_ref, rest_ref,
     tok, vectors, packed, field, patch, partial, w_big, mid, mine, plane_in, plane_sum, ring_in, direct_in,
     sel, gather, spread,
-    tok_sem, vec_sem, w_sem, mid_sem, send_sem, recv_sem, later_sem,
+    tok_sem, vec_sem, w_sem, mid_sem, send_sem, recv_sem,
     plane_send, plane_recv, ring_send, ring_recv, direct_send, direct_recv,
     know_x, know_all, know_first, know_plane,
 ):
@@ -76,7 +76,7 @@
         pltpu.make_async_copy(
             w_hbm,
             w_big.at[high, :, pl.ds(high, 3), pl.ds(16 * b, 48), pl.ds(channels * b, channels)],
-            w_sem.at[2 * high + b],
+            w_sem,
         )
         for high in (0, 1)
         for b in (0, 1)
@@ -84,7 +84,7 @@
     for copy in w_copies:
         copy.start()
     vector_copies = [
-        pltpu.make_async_copy(ref, vectors.at[i], vec_sem.at[i])
+        pltpu.make_async_copy(ref, vectors.at[i], vec_sem)
         for i, ref in enumerate((b_hbm, gain_hbm, shift_hbm, b_mid_hbm))
     ]
     for copy in vector_copies:
@@ -153,55 +153,84 @@
         + jnp.where(z == last, 1, 0)
     )
     pl.semaphore_wait(barrier, expected)
-    def tokens_copy(place, a, src_ta, to_ha, to_ta, slot, urgent):
-        there = pl.ds(src_ta * half, half)
+    def tokens_copy(place, a, to_ha, to_ta, send, arrival):
         frames = pl.ds(0, 2) if to_ta else pl.ds(1, 1)
         of = pl.ds(0, 2) if to_ta else pl.ds(0, 1)
         if a is None:
-            src, dst = packed.at[:, of], field.at[place, :, frames, there]
+            src, dst = packed.at[:, of], field.at[place, :, frames, own]
         else:
-            src, dst = packed.at[a, of], field.at[place, a, frames, there]
-        sem = recv_sem.at[place, src_ta] if urgent else later_sem.at[place // 2, src_ta]
+            src, dst = packed.at[a, of], field.at[place, a, frames, own]
         return pltpu.make_async_remote_copy(
-            src, dst, send_sem.at[slot], sem, device_id={"ha": to_ha, "ta": to_ta}, device_id_type=MESH
+            src, dst, send_sem.at[send], recv_sem.at[arrival],
+            device_id={"ha": to_ha, "ta": to_ta}, device_id_type=MESH,
         )
 
-    def each_token_copy(act, urgent):
+    def send_tokens(urgent):
         @pl.when(ha < n_ha - 1)
         def _():
             for t in (1, 0):
-                act(tokens_copy(0, int(urgent), ta, ha + 1, t, 2 * (1 - int(urgent)) + t, urgent))
+                tokens_copy(0, int(urgent), ha + 1, t, 0 if urgent else 3, 0 if urgent else 3).start()
 
         @pl.when(ha > 0)
         def _():
             for t in (1, 0):
-                act(tokens_copy(2, 1 - int(urgent), ta, ha - 1, t, 4 + 2 * (1 - int(urgent)) + t, urgent))
+                tokens_copy(2, 1 - int(urgent), ha - 1, t, 1 if urgent else 4, 2 if urgent else 4).start()
 
         if urgent:
             for t in (1, 0):
 
                 @pl.when(ta == 1 - t)
                 def _():
-                    act(tokens_copy(1, None, ta, ha, t, 8, True))
-
-    def each_token_arrival(act, urgent):
+                    tokens_copy(1, None, ha, t, 2, 1).start()
+
+    def await_tokens(urgent):
         for to_ta in (0, 1):
+            frames = pl.ds(0, 2) if to_ta else pl.ds(1, 1)
+
+            def arrived(ref, arrival):
+                pltpu.make_async_remote_copy(
+                    ref, ref, send_sem.at[2], recv_sem.at[arrival],
+                    device_id={"ha": ha, "ta": 1 - ta}, device_id_type=MESH,
+                ).wait_recv()
 
             @pl.when(ta == to_ta)
             def _():
                 if urgent is None:
-                    act(tokens_copy(1, None, 1 - to_ta, ha, to_ta, 8, True))
+                    arrived(field.at[1, :, frames, pl.ds((1 - to_ta) * half, half)], 1)
                     return
 
                 @pl.when(ha > 0)
                 def _():
-                    for t in (0, 1):
-                        act(tokens_copy(0, int(urgent), t, ha, to_ta, 0, urgent))
+                    arrived(field.at[0, int(urgent), frames], 0 if urgent else 3)
 
                 @pl.when(ha < n_ha - 1)
                 def _():
-                    for t in (0, 1):
-                        act(tokens_copy(2, 1 - int(urgent), t, ha, to_ta, 0, urgent))
+                    arrived(field.at[2, 1 - int(urgent), frames], 2 if urgent else 4)
+
+    def tokens_left():
+        three = field.at[pl.ds(0, 3), 0, 0, pl.ds(0, half)]
+
+        def left(ref, send):
+            pltpu.make_async_remote_copy(
+                ref, ref, send_sem.at[send], recv_sem.at[1],
+                device_id={"ha": ha, "ta": 1 - ta}, device_id_type=MESH,
+            ).wait_send()
+
+        @pl.when(ha < n_ha - 1)
+        def _():
+            left(three, 0)
+            left(three, 3)
+
+        @pl.when(ha > 0)
+        def _():
+            left(three, 1)
+            left(three, 4)
+
+        for t in (1, 0):
+
+            @pl.when(ta == 1 - t)
+            def _():
+                tokens_copy(1, None, ha, t, 2, 1).wait_send()
 
     def tell(sem, device):
         pl.semaphore_signal(sem, inc=1, device_id=device, device_id_type=MESH)
@@ -211,7 +240,7 @@
         for d in range(1, 1 + EARLY):
             tell(know_all, near(0, d, False))
 
-    each_token_copy(lambda copy: copy.start(), True)
+    send_tokens(True)
 
     tell(know_x, near(1, 0, False))
     tell(know_x, near(RING_X - 1, 0, False))
@@ -277,12 +306,11 @@
     k = lax.broadcasted_iota(jnp.int32, spread.shape, 0)
     n = lax.broadcasted_iota(jnp.int32, spread.shape, 1)
     spread[...] = jnp.where((n // members == k) & (k < 2 * GROUPS), 1.0, 0.0).astype(BF16)
-    for copy in vector_copies:
-        copy.wait()
+    pltpu.make_async_copy(vectors, vectors, vec_sem).wait()
     stat_ref[2:3] = vectors[3].reshape(1, -1)
-    for copy in w_copies:
-        copy.wait()
-    each_token_copy(lambda copy: copy.start(), False)
+    spread_over = w_big.at[:, :, pl.ds(0, 3), pl.ds(0, 48)]
+    pltpu.make_async_copy(spread_over, spread_over, w_sem).wait()
+    send_tokens(False)
 
     @pl.when(first)
     def _():
@@ -303,7 +331,7 @@
     tell_plane(0)
     tell_plane(1)
     pass_first((z == 2) | (z == 3), True)
-    each_token_arrival(lambda copy: copy.wait_recv(), None)
+    await_tokens(None)
     tokens = field.shape[3]
     row = lax.broadcasted_iota(jnp.int32, (tokens, 128), 0)
 
@@ -361,7 +389,7 @@
     patches(1, (0, 1))
     for y in (1, 2):
         partial[y - 1] = part_of_own(y, 1, bias)
-    each_token_arrival(lambda copy: copy.wait_recv(), True)
+    await_tokens(True)
     patches(0, (1,))
     patches(2, (0,))
     sums = jnp.zeros((1, 2 * channels), F32)
@@ -392,12 +420,12 @@
         @pl.when(late & where)
         def _():
             pl.semaphore_wait(know_plane.at[z0], 1)
-            for dx in (2, 1, 3, 0):
-                for flip in (1, 0):
-                    to = {"ha": (x + dx) % RING_X * RING_Z + z0, "ta": 1 - ta if flip else ta}
+            for to_x in range(RING_X):
+                for to_ta in (1, 0):
+                    slot = (last - z) * 8 + (to_x - x + RING_X) % RING_X * 2 + (to_ta + ta) % 2
                     pltpu.make_async_remote_copy(
-                        mine, direct_in.at[(last - z) * 8 + 2 * dx + flip], direct_send, direct_recv,
-                        device_id=to, device_id_type=MESH,
+                        mine, direct_in.at[slot], direct_send, direct_recv,
+                        device_id={"ha": to_x * RING_Z + z0, "ta": to_ta}, device_id_type=MESH,
                     ).start()
 
     direct_to(0, z >= last - 1)
@@ -417,7 +445,7 @@
     direct_to(0, z < last - 1)
     direct_to(1, True)
     pass_first(lower & (z >= 4), True)
-    each_token_arrival(lambda copy: copy.wait_recv(), False)
+    await_tokens(False)
     patches(0, (0, 1))
     patches(2, (0, 1))
     hidden_rows(0, 0, 6)
@@ -474,8 +502,7 @@
     def _():
         for p in range(3):
             transform(p)
-    each_token_copy(lambda copy: copy.wait_send(), True)
-    each_token_copy(lambda copy: copy.wait_send(), False)
+    tokens_left()
     all_plane.wait_send()
     def ring_copies(number):
         return pltpu.make_async_remote_copy(
@@ -610,7 +637,7 @@
     def send(y, f):
         for part in range(parts):
             out[f, y, :, 128 * part : 128 * part + 128] = rows_f32[y, f, part].astype(BF16)
-        copies.append(pltpu.make_async_copy(out.at[f, y], out_hbm.at[f, y], out_sem.at[frames * y + f]))
+        copies.append(pltpu.make_async_copy(out.at[f, y], out_hbm.at[f, y], out_sem))
         copies[-1].start()
 
     def combine(i, f):
@@ -670,8 +697,7 @@
                 ]
     for f in range(frames):
         last_odd(f)
-    for copy in copies:
-        copy.wait()
+    pltpu.make_async_copy(out, out_hbm, out_sem).wait()
 
 
 def keep(value):
@@ -716,12 +742,11 @@
             pltpu.VMEM((2 * channels, 128), BF16),
             pltpu.VMEM((128, 2 * channels), BF16),
             pltpu.SemaphoreType.DMA,
-            pltpu.SemaphoreType.DMA((4,)),
-            pltpu.SemaphoreType.DMA((4,)),
+            pltpu.SemaphoreType.DMA,
+            pltpu.SemaphoreType.DMA,
             pltpu.SemaphoreType.DMA((3,)),
-            pltpu.SemaphoreType.DMA((9,)),
-            pltpu.SemaphoreType.DMA((3, 2)),
-            pltpu.SemaphoreType.DMA((2, 2)),
+            pltpu.SemaphoreType.DMA((5,)),
+            pltpu.SemaphoreType.DMA((5,)),
             pltpu.SemaphoreType.DMA,
             pltpu.SemaphoreType.DMA,
             pltpu.SemaphoreType.DMA,
@@ -753,7 +778,7 @@
             pltpu.VMEM((2, 2, 4, parts, tokens, 128), F32),
             pltpu.VMEM((2, 4, parts, 2 * tokens, 128), F32),
             pltpu.VMEM((4, 2, 2 * tokens, channels), BF16),
-            pltpu.SemaphoreType.DMA((8,)),
+            pltpu.SemaphoreType.DMA,
         ],
         compiler_params=pltpu.CompilerParams(vmem_limit_bytes=28 * 2**20),
         name="decode",

time: 43 us -> 42.8 us (level)
  no operation moved by 1% of the time
where the time goes in v5:
time: 42.8 us; the launch traced here: 42.6 us
  Pallas kernels  42.5 us (99%)
    pallas_call x1, Pallas kernels, body(): pl.pallas_call(exchange_kernel, out_shape=(jax.ShapeDtypeStruct((6, 4, 2...  35.3 us
    pallas_call x1, Pallas kernels, body(): pl.pallas_call(decode_kernel, out_shape=jax.ShapeDtypeStruct((4, 2, 2 * t...  7.21 us

profile of v5, /device:TPU:33, one launch (start us, length us, event | category | flops | bytes accessed | tf_op | source)
XLA Modules:
  0.0 42.6 jit_solution(7154396050622107615)
XLA Ops:
  0.0 35.3 %exchange.1 = (f32[6,4,6,64,128]{4,3,2,1,0:T(8,128)S(1)}, f32[3,384]{1,0:T(4,128)S(1)}, bf16[16,1152,256]{2,1,0:T(8,128)(2,1)S(1)}, bf16[16,1536,256]{2,1,0:T(8,128)(2,1)S(1)}) custom-call(bf16[8,32,64]{2,1,0:T(8,128)(2,1)} %tok_hbm.1, bf16[3,3,48,384]{3,2,1,0:T(8,128)(2,1)} %bitcast.1, f32[384]{0:T(512)} %b_hbm.1, f32[384]{0:T(512)} %gain_hbm.1, ...), custom_call_target="tpu_custom_call" | custom-call | tf_op jit(solution)/shard_map/exchange/pallas_call | solution.py:717
  35.3 7.2 %decode.1 = bf16[4,2,128,384]{3,2,1,0:T(8,128)(2,1)} custom-call(f32[6,4,6,64,128]{4,3,2,1,0:T(8,128)S(1)} %get-tuple-element.9.h_ref, f32[3,384]{1,0:T(4,128)S(1)} %get-tuple-element.10.stat_ref, bf16[16,1152,256]{2,1,0:T(8,128)(2,1)S(1)} %get-tuple-element.11.main_ref, bf16[16,1536,256]{2,1,0:T(8,128)(2,1)S(1)} %get-tuple-element.12.rest_ref), custom_call_target="tpu_custom_call" | custom-call | tf_op jit(solution)/shard_map/decode/pallas_call | solution.py:766

commit v6 on v5

--- a/solution.py
+++ b/solution.py
@@ -168,12 +168,12 @@
     def send_tokens(urgent):
         @pl.when(ha < n_ha - 1)
         def _():
-            for t in (1, 0):
+            for t in (0, 1):
                 tokens_copy(0, int(urgent), ha + 1, t, 0 if urgent else 3, 0 if urgent else 3).start()
 
         @pl.when(ha > 0)
         def _():
-            for t in (1, 0):
+            for t in (0, 1):
                 tokens_copy(2, 1 - int(urgent), ha - 1, t, 1 if urgent else 4, 2 if urgent else 4).start()
 
         if urgent:

time: 42.8 us -> 42.7 us (level)
  no operation moved by 1% of the time
where the time goes in v6:
time: 42.7 us; the launch traced here: 42.6 us
  Pallas kernels  42.5 us (100%)
    pallas_call x1, Pallas kernels, body(): pl.pallas_call(exchange_kernel, out_shape=(jax.ShapeDtypeStruct((6, 4, 2...  35.3 us
    pallas_call x1, Pallas kernels, body(): pl.pallas_call(decode_kernel, out_shape=jax.ShapeDtypeStruct((4, 2, 2 * t...  7.21 us

profile of v6, /device:TPU:33, one launch (start us, length us, event | category | flops | bytes accessed | tf_op | source)
XLA Modules:
  0.0 42.6 jit_solution(6964771200220004335)
XLA Ops:
  0.0 35.3 %exchange.1 = (f32[6,4,6,64,128]{4,3,2,1,0:T(8,128)S(1)}, f32[3,384]{1,0:T(4,128)S(1)}, bf16[16,1152,256]{2,1,0:T(8,128)(2,1)S(1)}, bf16[16,1536,256]{2,1,0:T(8,128)(2,1)S(1)}) custom-call(bf16[8,32,64]{2,1,0:T(8,128)(2,1)} %tok_hbm.1, bf16[3,3,48,384]{3,2,1,0:T(8,128)(2,1)} %bitcast.1, f32[384]{0:T(512)} %b_hbm.1, f32[384]{0:T(512)} %gain_hbm.1, ...), custom_call_target="tpu_custom_call" | custom-call | tf_op jit(solution)/shard_map/exchange/pallas_call | solution.py:717
  35.3 7.2 %decode.1 = bf16[4,2,128,384]{3,2,1,0:T(8,128)(2,1)} custom-call(f32[6,4,6,64,128]{4,3,2,1,0:T(8,128)S(1)} %get-tuple-element.9.h_ref, f32[3,384]{1,0:T(4,128)S(1)} %get-tuple-element.10.stat_ref, bf16[16,1152,256]{2,1,0:T(8,128)(2,1)S(1)} %get-tuple-element.11.main_ref, bf16[16,1536,256]{2,1,0:T(8,128)(2,1)S(1)} %get-tuple-element.12.rest_ref), custom_call_target="tpu_custom_call" | custom-call | tf_op jit(solution)/shard_map/decode/pallas_call | solution.py:766

commit v7 on v5

--- a/solution.py
+++ b/solution.py
@@ -598,8 +598,9 @@
         for f in range(frames_in):
             value = jnp.concatenate([one(f, part) for part in range(wide // 128)], axis=-1)
             columns_wide[k, f, y] = value.astype(BF16)
-            value = jnp.concatenate([one(f, part) for part in range(wide // 128, parts)], axis=-1)
-            columns_rest[k, f, y] = value.astype(BF16)
+        for f in range(0, frames_in, 2):
+            value = jnp.concatenate([one(f, parts - 1), one(f + 1, parts - 1)], axis=-1)
+            columns_rest[k, f // 2, y] = value.astype(BF16)
 
     def by_rows(i, k):
         one, two = ((0, 2), (1, 2), (2, 1), (1, 3))[i]
@@ -679,15 +680,18 @@
             if at == 15:
                 for f in range(frames):
                     last_even(f)
-            both = (planes_wide.at[k % 2], planes_rest.at[k % 2])
-            lhs = [planes[p : p + frames] for p in range(3) for planes in both]
-            lhs = jnp.concatenate(lhs, axis=-1).reshape(frames * tokens, 3 * channels)
+            def plane(f):
+                last = planes_rest[k % 2, f // 2, :, rest * (f % 2) : rest * (f % 2) + rest]
+                return jnp.concatenate([planes_wide[k % 2, f], last], axis=-1)
+
+            lhs = [jnp.concatenate([plane(f + p) for p in range(3)], axis=-1) for f in range(frames)]
+            lhs = jnp.concatenate(lhs, axis=0)
             product = jnp.dot(lhs, main_ref[at], preferred_element_type=F32)
             held["product"] = 0.0 * product[0:1, 0:128]
             for part in range(wide // 128):
                 products[i % 2, k, :, part] = product[:, 128 * part : 128 * part + 128].reshape(frames, tokens, 128)
             lhs = [
-                jnp.concatenate([planes[t + p] for p in range(4) for planes in both], axis=-1)
+                jnp.concatenate([plane(t + p) for p in range(4)], axis=-1)
                 for t in range(0, frames, 2)
             ]
             product = jnp.dot(jnp.concatenate(lhs, axis=0), rest_ref[at], preferred_element_type=F32)
@@ -771,9 +775,9 @@
         scratch_shapes=[
             pltpu.VMEM((6, parts, 4, 2, tokens + 16, 128), F32),
             pltpu.VMEM((4, 6, 4, tokens, wide), BF16),
-            pltpu.VMEM((4, 6, 4, tokens, rest), BF16),
+            pltpu.VMEM((4, 3, 4, tokens, 2 * rest), BF16),
             pltpu.VMEM((2, 6, tokens, wide), BF16),
-            pltpu.VMEM((2, 6, tokens, rest), BF16),
+            pltpu.VMEM((2, 3, tokens, 2 * rest), BF16),
             pltpu.VMEM((2, 4, 4, parts, tokens, 128), F32),
             pltpu.VMEM((2, 2, 4, parts, tokens, 128), F32),
             pltpu.VMEM((2, 4, parts, 2 * tokens, 128), F32),

time: 42.8 us -> 42.7 us (level)
  no operation moved by 1% of the time
where the time goes in v7:
time: 42.7 us; the launch traced here: 42.6 us
  Pallas kernels  42.4 us (99%)
    pallas_call x1, Pallas kernels, body(): pl.pallas_call(exchange_kernel, out_shape=(jax.ShapeDtypeStruct((6, 4, 2...  35.3 us
    pallas_call x1, Pallas kernels, body(): pl.pallas_call(decode_kernel, out_shape=jax.ShapeDtypeStruct((4, 2, 2 * t...  7.12 us

profile of v7, /device:TPU:33, one launch (start us, length us, event | category | flops | bytes accessed | tf_op | source)
XLA Modules:
  0.0 42.6 jit_solution(5744527261026178556)
XLA Ops:
  0.0 35.3 %exchange.1 = (f32[6,4,6,64,128]{4,3,2,1,0:T(8,128)S(1)}, f32[3,384]{1,0:T(4,128)S(1)}, bf16[16,1152,256]{2,1,0:T(8,128)(2,1)S(1)}, bf16[16,1536,256]{2,1,0:T(8,128)(2,1)S(1)}) custom-call(bf16[8,32,64]{2,1,0:T(8,128)(2,1)} %tok_hbm.1, bf16[3,3,48,384]{3,2,1,0:T(8,128)(2,1)} %bitcast.1, f32[384]{0:T(512)} %b_hbm.1, f32[384]{0:T(512)} %gain_hbm.1, ...), custom_call_target="tpu_custom_call" | custom-call | tf_op jit(solution)/shard_map/exchange/pallas_call | solution.py:721
  35.3 7.1 %decode.1 = bf16[4,2,128,384]{3,2,1,0:T(8,128)(2,1)} custom-call(f32[6,4,6,64,128]{4,3,2,1,0:T(8,128)S(1)} %get-tuple-element.9.h_ref, f32[3,384]{1,0:T(4,128)S(1)} %get-tuple-element.10.stat_ref, bf16[16,1152,256]{2,1,0:T(8,128)(2,1)S(1)} %get-tuple-element.11.main_ref, bf16[16,1536,256]{2,1,0:T(8,128)(2,1)S(1)} %get-tuple-element.12.rest_ref), custom_call_target="tpu_custom_call" | custom-call | tf_op jit(solution)/shard_map/decode/pallas_call | solution.py:770

commit v8 on v7

--- a/solution.py
+++ b/solution.py
@@ -1,3 +1,5 @@
+import functools
+
 import jax
 import jax.numpy as jnp
 from jax import lax
@@ -22,7 +24,7 @@
     tok, vectors, packed, field, patch, partial, w_big, mid, mine, plane_in, plane_sum, ring_in, direct_in,
     sel, gather, spread,
     tok_sem, vec_sem, w_sem, mid_sem, send_sem, recv_sem,
-    plane_send, plane_recv, ring_send, ring_recv, direct_send, direct_recv,
+    sums_send, plane_recv, ring_recv, direct_recv,
     know_x, know_all, know_first, know_plane,
 ):
     ha, ta = lax.axis_index("ha"), lax.axis_index("ta")
@@ -37,7 +39,7 @@
         hz = (z + dz) % RING_Z
         return {"ha": hx * RING_Z + hz, "ta": 1 - ta if flip else ta}
     ring_in[...] = jnp.zeros_like(ring_in)
-    direct_in[...] = jnp.zeros_like(direct_in)
+    direct_in[0 : 8 * LATE] = jnp.zeros_like(direct_in[0 : 8 * LATE])
     barrier = pltpu.get_barrier_semaphore()
 
     def greet(device):
@@ -106,7 +108,7 @@
     def transform(p):
         fetch(p).wait()
 
-        def rows(step, carry):
+        def rows(moved, step, carry):
             at = pl.multiple_of(step * 16, 16)
             for part in range(parts):
                 lanes = slice(128 * part, 128 * part + 128)
@@ -115,14 +117,20 @@
                 for i in range(4):
                     for k, value in enumerate(bank(*[by_row[r][i] for r in range(3)])):
                         value = value.astype(BF16)
-                        if 128 * part < wide:
-                            main_ref[4 * i + k, pl.ds(at + p * channels, 16), lanes] = value
-                        else:
+                        if 128 * part >= wide:
                             rest_ref[4 * i + k, pl.ds(at + p * channels, 16), :rest] = value
                             rest_ref[4 * i + k, pl.ds(at + (p + 1) * channels, 16), rest:] = value
+                        elif moved and i and k == 2:
+                            for other in (0, 3):
+                                main_ref[4 * i + other, pl.ds(at + 3 * channels - wide, 16), lanes] = value
+                        else:
+                            main_ref[4 * i + k, pl.ds(at + p * channels, 16), lanes] = value
             return carry
 
-        lax.fori_loop(0, channels // 16, rows, 0)
+        end = wide // 16 if p == 2 else channels // 16
+        lax.fori_loop(0, end, functools.partial(rows, False), 0)
+        if p == 2:
+            lax.fori_loop(end, channels // 16, functools.partial(rows, True), 0)
 
     early = z < 2
     lower = z < RING_Z // 2
@@ -153,7 +161,7 @@
         + jnp.where(z == last, 1, 0)
     )
     pl.semaphore_wait(barrier, expected)
-    def tokens_copy(place, a, to_ha, to_ta, send, arrival):
+    def tokens_copy(place, a, to_ha, to_ta, arrival):
         frames = pl.ds(0, 2) if to_ta else pl.ds(1, 1)
         of = pl.ds(0, 2) if to_ta else pl.ds(0, 1)
         if a is None:
@@ -161,7 +169,7 @@
         else:
             src, dst = packed.at[a, of], field.at[place, a, frames, own]
         return pltpu.make_async_remote_copy(
-            src, dst, send_sem.at[send], recv_sem.at[arrival],
+            src, dst, send_sem, recv_sem.at[arrival],
             device_id={"ha": to_ha, "ta": to_ta}, device_id_type=MESH,
         )
 
@@ -169,19 +177,21 @@
         @pl.when(ha < n_ha - 1)
         def _():
             for t in (1, 0):
-                tokens_copy(0, int(urgent), ha + 1, t, 0 if urgent else 3, 0 if urgent else 3).start()
+                tokens_copy(0, int(urgent), ha + 1, t, 1 if urgent else 2).start()
 
         @pl.when(ha > 0)
         def _():
             for t in (1, 0):
-                tokens_copy(2, 1 - int(urgent), ha - 1, t, 1 if urgent else 4, 2 if urgent else 4).start()
+                tokens_copy(2, 1 - int(urgent), ha - 1, t, 1 if urgent else 2).start()
 
         if urgent:
             for t in (1, 0):
 
                 @pl.when(ta == 1 - t)
                 def _():
-                    tokens_copy(1, None, ha, t, 2, 1).start()
+                    tokens_copy(1, None, ha, t, 0).start()
+
+    inner = (ha > 0) & (ha < n_ha - 1)
 
     def await_tokens(urgent):
         for to_ta in (0, 1):
@@ -189,48 +199,38 @@
 
             def arrived(ref, arrival):
                 pltpu.make_async_remote_copy(
-                    ref, ref, send_sem.at[2], recv_sem.at[arrival],
+                    ref, ref, send_sem, recv_sem.at[arrival],
                     device_id={"ha": ha, "ta": 1 - ta}, device_id_type=MESH,
                 ).wait_recv()
 
-            @pl.when(ta == to_ta)
+            if urgent is None:
+
+                @pl.when(ta == to_ta)
+                def _():
+                    arrived(field.at[1, :, frames, pl.ds((1 - to_ta) * half, half)], 0)
+
+            else:
+
+                @pl.when((ta == to_ta) & inner)
+                def _():
+                    arrived(field.at[0, :, frames], 1 if urgent else 2)
+
+                @pl.when((ta == to_ta) & jnp.logical_not(inner))
+                def _():
+                    arrived(field.at[0, 0, frames], 1 if urgent else 2)
+
+    def tokens_left():
+        for to_ta, blocks, where in ((1, 16, inner), (0, 14, inner)) + tuple(
+            (t, n, jnp.logical_not(inner)) for t, n in ((1, 10), (0, 8))
+        ):
+
+            @pl.when(where & (ta == 1 - to_ta))
             def _():
-                if urgent is None:
-                    arrived(field.at[1, :, frames, pl.ds((1 - to_ta) * half, half)], 1)
-                    return
-
-                @pl.when(ha > 0)
-                def _():
-                    arrived(field.at[0, int(urgent), frames], 0 if urgent else 3)
-
-                @pl.when(ha < n_ha - 1)
-                def _():
-                    arrived(field.at[2, 1 - int(urgent), frames], 2 if urgent else 4)
-
-    def tokens_left():
-        three = field.at[pl.ds(0, 3), 0, 0, pl.ds(0, half)]
-
-        def left(ref, send):
-            pltpu.make_async_remote_copy(
-                ref, ref, send_sem.at[send], recv_sem.at[1],
-                device_id={"ha": ha, "ta": 1 - ta}, device_id_type=MESH,
-            ).wait_send()
-
-        @pl.when(ha < n_ha - 1)
-        def _():
-            left(three, 0)
-            left(three, 3)
-
-        @pl.when(ha > 0)
-        def _():
-            left(three, 1)
-            left(three, 4)
-
-        for t in (1, 0):
-
-            @pl.when(ta == 1 - t)
-            def _():
-                tokens_copy(1, None, ha, t, 2, 1).wait_send()
+                gone = patch.at[pl.ds(0, blocks // 2), 0]
+                pltpu.make_async_remote_copy(
+                    gone, gone, send_sem, recv_sem.at[0],
+                    device_id={"ha": ha, "ta": 1 - ta}, device_id_type=MESH,
+                ).wait_send()
 
     def tell(sem, device):
         pl.semaphore_signal(sem, inc=1, device_id=device, device_id_type=MESH)
@@ -302,10 +302,10 @@
                 sel[384 * a + 128 * step + lanes * f : 384 * a + 128 * step + lanes * (f + 1), 128 * f : 128 * f + 128] = block
     k = lax.broadcasted_iota(jnp.int32, gather.shape, 0)
     n = lax.broadcasted_iota(jnp.int32, gather.shape, 1)
-    gather[...] = jnp.where((k // members == n) & (n < 2 * GROUPS), 1.0, 0.0).astype(BF16)
+    gather[...] = jnp.where((k // members == n % GROUPS) & (n < 2 * GROUPS), 1.0, 0.0).astype(BF16)
     k = lax.broadcasted_iota(jnp.int32, spread.shape, 0)
     n = lax.broadcasted_iota(jnp.int32, spread.shape, 1)
-    spread[...] = jnp.where((n // members == k) & (k < 2 * GROUPS), 1.0, 0.0).astype(BF16)
+    spread[...] = jnp.where((n // members == k % GROUPS) & (k < 2 * GROUPS), 1.0, 0.0).astype(BF16)
     pltpu.make_async_copy(vectors, vectors, vec_sem).wait()
     stat_ref[2:3] = vectors[3].reshape(1, -1)
     spread_over = w_big.at[:, :, pl.ds(0, 3), pl.ds(0, 48)]
@@ -399,20 +399,20 @@
         keep_hidden(y, 2, 4, values)
         sums = sums + jnp.sum(values, axis=0, keepdims=True)
         squares = squares + jnp.sum(values * values, axis=0, keepdims=True)
-    def product(value, matrix):
+    def product(values, matrix):
         terms = []
-        for _ in range(3):
-            term = value.astype(BF16)
-            terms.append(term.astype(F32))
-            value = value - terms[-1]
-        terms = jnp.concatenate(terms + [jnp.zeros((5, value.shape[1]), F32)], axis=0).astype(BF16)
+        for value in values:
+            for _ in range(3):
+                term = value.astype(BF16)
+                terms.append(term.astype(F32))
+                value = value - terms[-1]
+        terms = jnp.concatenate(terms + [jnp.zeros((2, values[0].shape[1]), F32)], axis=0).astype(BF16)
         result = jnp.dot(terms, matrix, preferred_element_type=F32)
-        return result[0:1] + result[1:2] + result[2:3]
-
-    folded = jnp.concatenate(
-        [both[:, :channels] + both[:, channels:] for both in (sums, squares)], axis=-1
-    )
-    mine[...] = product(folded, gather[...])
+        return [result[at : at + 1] + result[at + 1 : at + 2] + result[at + 2 : at + 3] for at in (0, 3)]
+
+    folded = [both[:, :channels] + both[:, channels:] for both in (sums, squares)]
+    of_sums = lax.broadcasted_iota(jnp.int32, (1, 128), 1) < GROUPS
+    mine[...] = jnp.where(of_sums, *product(folded, gather[...]))
     @pl.when(z > 1)
     def _():
         pl.semaphore_wait(know_x, 2)
@@ -424,7 +424,7 @@
                 for to_ta in (1, 0):
                     slot = (last - z) * 8 + (to_x - x + RING_X) % RING_X * 2 + (to_ta + ta) % 2
                     pltpu.make_async_remote_copy(
-                        mine, direct_in.at[slot], direct_send, direct_recv,
+                        mine, direct_in.at[slot], sums_send, direct_recv,
                         device_id={"ha": to_x * RING_Z + z0, "ta": to_ta}, device_id_type=MESH,
                     ).start()
 
@@ -436,7 +436,7 @@
                 slot = 2 * dx + flip - 1
                 plane.append(
                     pltpu.make_async_remote_copy(
-                        mine, plane_in.at[slot], plane_send, plane_recv,
+                        mine, plane_in.at[slot], sums_send, plane_recv,
                         device_id=near(dx, 0, bool(flip)), device_id_type=MESH,
                     )
                 )
@@ -457,7 +457,7 @@
         direct_to(z0, True)
     total = mine[...]
     all_plane = pltpu.make_async_remote_copy(
-        plane_in, plane_in, plane_send, plane_recv, device_id=near(0, 0, True), device_id_type=MESH
+        plane_in, plane_in, sums_send, plane_recv, device_id=near(0, 0, True), device_id_type=MESH
     )
     all_plane.wait_recv()
     for slot in range(plane_in.shape[0]):
@@ -465,7 +465,7 @@
     plane_sum[...] = total
     def ring_copy(d):
         return pltpu.make_async_remote_copy(
-            plane_sum, ring_in.at[d - 1], ring_send, ring_recv,
+            plane_sum, ring_in.at[d - 1], sums_send, ring_recv,
             device_id=near(0, d, False), device_id_type=MESH,
         )
 
@@ -503,16 +503,15 @@
         for p in range(3):
             transform(p)
     tokens_left()
-    all_plane.wait_send()
     def ring_copies(number):
         return pltpu.make_async_remote_copy(
-            ring_in.at[pl.ds(0, number)], ring_in.at[pl.ds(0, number)], ring_send, ring_recv,
+            ring_in.at[pl.ds(0, number)], ring_in.at[pl.ds(0, number)], sums_send, ring_recv,
             device_id=near(0, 1, False), device_id_type=MESH,
         )
 
     def direct_copies(number):
         return pltpu.make_async_remote_copy(
-            direct_in.at[pl.ds(0, number)], direct_in.at[pl.ds(0, number)], direct_send, direct_recv,
+            direct_in.at[pl.ds(0, number)], direct_in.at[pl.ds(0, number)], sums_send, direct_recv,
             device_id=near(0, 1, False), device_id_type=MESH,
         )
 
@@ -534,21 +533,22 @@
         rows = [sum(rows[at + 1 : at + 2], rows[at]) for at in range(0, len(rows), 2)]
     total = total + rows[0]
     count = n_ha * lax.axis_size("ta") * 4 * 2 * 2 * tokens * members
-    shared = product(total * (1.0 / count), spread[...])
-    mean, square = shared[:, :channels], shared[:, channels:]
+    total = total * (1.0 / count)
+    mean, square = product((jnp.where(of_sums, total, 0.0), jnp.where(of_sums, 0.0, total)), spread[...])
     var = jnp.maximum(square - mean * mean, 0.0)
     scale = lax.rsqrt(var + EPS) * vectors[1].reshape(1, -1)
     stat_ref[0:1] = 0.5 * scale
     stat_ref[1:2] = 0.5 * (vectors[2].reshape(1, -1) - mean * scale)
 
+    by_late = len(plane) + last - EARLY + 8 * EARLY
+
     @pl.when(late)
     def _():
-        ring_copies(last - EARLY).wait_send()
-        direct_copies(8 * EARLY).wait_send()
+        direct_copies(by_late).wait_send()
 
     @pl.when(jnp.logical_not(late))
     def _():
-        ring_copies(last).wait_send()
+        direct_copies(len(plane) + last).wait_send()
 
 
 def decode_kernel(
@@ -602,13 +602,16 @@
             value = jnp.concatenate([one(f, parts - 1), one(f + 1, parts - 1)], axis=-1)
             columns_rest[k, f // 2, y] = value.astype(BF16)
 
+    order = [(i, k) for i in range(4) for k in ((1, 2, 0, 3) if i else range(4))]
+    slot_of = {pair: step % 2 for step, pair in enumerate(order)}
+
     def by_rows(i, k):
         one, two = ((0, 2), (1, 2), (2, 1), (1, 3))[i]
-        for columns, planes in ((columns_wide, planes_wide), (columns_rest, planes_rest)):
+        for columns, planes, slot in ((columns_wide, planes_wide, slot_of[i, k]), (columns_rest, planes_rest, k)):
             if i == 1:
-                planes[k % 2] = columns[k, :, one] + columns[k, :, two]
+                planes[slot] = columns[k, :, one] + columns[k, :, two]
             else:
-                planes[k % 2] = columns[k, :, one] - columns[k, :, two]
+                planes[slot] = columns[k, :, one] - columns[k, :, two]
 
     ahead = {
         0: [(activate, 0, 0), (activate, 2, 0), (by_columns, 0, 1), (by_columns, 2, 1)],
@@ -667,26 +670,32 @@
             done(1, 1, f, part, total[1, 1, f, part] + products[1, 3, f, part])
         send(1, f)
 
-    for i in range(4):
-        for k in range(4):
+    for step, (i, k) in enumerate(order):
             at = 4 * i + k
-            for make, one, two in ahead.get(at, ()):
+            for make, one, two in ahead.get(step, ()):
                 make(one, two)
-            if at < 15:
-                by_rows((at + 1) // 4, (at + 1) % 4)
-            if i and k < 2:
-                combine(i - 1, 2 * k)
-                combine(i - 1, 2 * k + 1)
-            if at == 15:
+            if step < 15:
+                by_rows(*order[step + 1])
+            if i and step % 4 < 2:
+                combine(i - 1, 2 * (step % 4))
+                combine(i - 1, 2 * (step % 4) + 1)
+            if step == 15:
                 for f in range(frames):
                     last_even(f)
+
+            def last_channels(f, k):
+                return planes_rest[k, f // 2, :, rest * (f % 2) : rest * (f % 2) + rest]
+
             def plane(f):
-                last = planes_rest[k % 2, f // 2, :, rest * (f % 2) : rest * (f % 2) + rest]
-                return jnp.concatenate([planes_wide[k % 2, f], last], axis=-1)
-
-            lhs = [jnp.concatenate([plane(f + p) for p in range(3)], axis=-1) for f in range(frames)]
-            lhs = jnp.concatenate(lhs, axis=0)
-            product = jnp.dot(lhs, main_ref[at], preferred_element_type=F32)
+                return jnp.concatenate([planes_wide[slot_of[i, k], f], last_channels(f, k)], axis=-1)
+
+            lhs = [[plane(f + p) for p in range(3)] for f in range(frames)]
+            if i and k in (0, 3):
+                lhs = [taps + [last_channels(f + 2, 2)] for f, taps in enumerate(lhs)]
+            lhs = jnp.concatenate([jnp.concatenate(taps, axis=-1) for taps in lhs], axis=0)
+            if i and k == 2:
+                lhs = lhs[:, : 3 * channels - rest]
+            product = jnp.dot(lhs, main_ref[at, : lhs.shape[1]], preferred_element_type=F32)
             held["product"] = 0.0 * product[0:1, 0:128]
             for part in range(wide // 128):
                 products[i % 2, k, :, part] = product[:, 128 * part : 128 * part + 128].reshape(frames, tokens, 128)
@@ -723,7 +732,7 @@
         out_shape=(
             jax.ShapeDtypeStruct((6, 4, 2 * parts, tokens, 128), F32),
             jax.ShapeDtypeStruct((3, channels), F32),
-            jax.ShapeDtypeStruct((16, 3 * channels, wide), BF16),
+            jax.ShapeDtypeStruct((16, 3 * channels + rest, wide), BF16),
             jax.ShapeDtypeStruct((16, 4 * channels, 2 * rest), BF16),
         ),
         in_specs=[hbm] * len(inputs),
@@ -741,18 +750,16 @@
             pltpu.VMEM((7, 1, 128), F32),
             pltpu.VMEM((1, 128), F32),
             pltpu.VMEM((RING_Z - 1, 1, 128), F32),
-            pltpu.VMEM((8 * max(LATE, EARLY), 1, 128), F32),
+            pltpu.VMEM((max(8 * LATE, 2 * RING_X - 1 + RING_Z - 1 + 7 * EARLY), 1, 128), F32),
             pltpu.VMEM((2 * 384, 4 * 128), BF16),
-            pltpu.VMEM((2 * channels, 128), BF16),
-            pltpu.VMEM((128, 2 * channels), BF16),
+            pltpu.VMEM((channels, 128), BF16),
+            pltpu.VMEM((128, channels), BF16),
             pltpu.SemaphoreType.DMA,
             pltpu.SemaphoreType.DMA,
             pltpu.SemaphoreType.DMA,
             pltpu.SemaphoreType.DMA((3,)),
-            pltpu.SemaphoreType.DMA((5,)),
-            pltpu.SemaphoreType.DMA((5,)),
             pltpu.SemaphoreType.DMA,
-            pltpu.SemaphoreType.DMA,
+            pltpu.SemaphoreType.DMA((3,)),
             pltpu.SemaphoreType.DMA,
             pltpu.SemaphoreType.DMA,
             pltpu.SemaphoreType.DMA,
@@ -763,7 +770,7 @@
             pltpu.SemaphoreType.REGULAR((EARLY,)),
         ],
         compiler_params=pltpu.CompilerParams(
-            collective_id=0, has_side_effects=True, vmem_limit_bytes=20 * 2**20
+            collective_id=0, has_side_effects=True, vmem_limit_bytes=18 * 2**20
         ),
         name="exchange",
     )(*[keep(value) for value in inputs])
@@ -777,14 +784,14 @@
             pltpu.VMEM((4, 6, 4, tokens, wide), BF16),
             pltpu.VMEM((4, 3, 4, tokens, 2 * rest), BF16),
             pltpu.VMEM((2, 6, tokens, wide), BF16),
-            pltpu.VMEM((2, 3, tokens, 2 * rest), BF16),
+            pltpu.VMEM((4, 3, tokens, 2 * rest), BF16),
             pltpu.VMEM((2, 4, 4, parts, tokens, 128), F32),
             pltpu.VMEM((2, 2, 4, parts, tokens, 128), F32),
             pltpu.VMEM((2, 4, parts, 2 * tokens, 128), F32),
             pltpu.VMEM((4, 2, 2 * tokens, channels), BF16),
             pltpu.SemaphoreType.DMA,
         ],
-        compiler_params=pltpu.CompilerParams(vmem_limit_bytes=28 * 2**20),
+        compiler_params=pltpu.CompilerParams(vmem_limit_bytes=22 * 2**20),
         name="decode",
     )(*prepared)
 

time: 42.7 us -> 42.4 us (level)
  no operation moved by 1% of the time
where the time goes in v8:
time: 42.4 us; the launch traced here: 42.2 us
  Pallas kernels  42.1 us (99%)
    pallas_call x1, Pallas kernels, body(): pl.pallas_call(exchange_kernel, out_shape=(jax.ShapeDtypeStruct((6, 4, 2...  35.2 us
    pallas_call x1, Pallas kernels, body(): pl.pallas_call(decode_kernel, out_shape=jax.ShapeDtypeStruct((4, 2, 2 * t...  6.88 us

profile of v8, /device:TPU:33, one launch (start us, length us, event | category | flops | bytes accessed | tf_op | source)
XLA Modules:
  0.0 42.2 jit_solution(14459643427267732377)
XLA Ops:
  0.0 35.2 %exchange.1 = (f32[6,4,6,64,128]{4,3,2,1,0:T(8,128)S(1)}, f32[3,384]{1,0:T(4,128)S(1)}, bf16[16,1280,256]{2,1,0:T(8,128)(2,1)S(1)}, bf16[16,1536,256]{2,1,0:T(8,128)(2,1)S(1)}) custom-call(bf16[8,32,64]{2,1,0:T(8,128)(2,1)} %tok_hbm.1, bf16[3,3,48,384]{3,2,1,0:T(8,128)(2,1)} %bitcast.1, f32[384]{0:T(512)} %b_hbm.1, f32[384]{0:T(512)} %gain_hbm.1, ...), custom_call_target="tpu_custom_call" | custom-call | tf_op jit(solution)/shard_map/exchange/pallas_call | solution.py:730
  35.2 6.9 %decode.1 = bf16[4,2,128,384]{3,2,1,0:T(8,128)(2,1)} custom-call(f32[6,4,6,64,128]{4,3,2,1,0:T(8,128)S(1)} %get-tuple-element.9.h_ref, f32[3,384]{1,0:T(4,128)S(1)} %get-tuple-element.10.stat_ref, bf16[16,1280,256]{2,1,0:T(8,128)(2,1)S(1)} %get-tuple-element.11.main_ref, bf16[16,1536,256]{2,1,0:T(8,128)(2,1)S(1)} %get-tuple-element.12.rest_ref), custom_call_target="tpu_custom_call" | custom-call | tf_op jit(solution)/shard_map/decode/pallas_call | solution.py:777

commit v9 on v8

--- a/solution.py
+++ b/solution.py
@@ -176,12 +176,12 @@
     def send_tokens(urgent):
         @pl.when(ha < n_ha - 1)
         def _():
-            for t in (1, 0):
+            for t in (0, 1):
                 tokens_copy(0, int(urgent), ha + 1, t, 1 if urgent else 2).start()
 
         @pl.when(ha > 0)
         def _():
-            for t in (1, 0):
+            for t in (0, 1):
                 tokens_copy(2, 1 - int(urgent), ha - 1, t, 1 if urgent else 2).start()
 
         if urgent:

time: 42.4 us -> 42.3 us (level)
  no operation moved by 1% of the time
where the time goes in v9:
time: 42.3 us; the launch traced here: 42.2 us
  Pallas kernels  42.1 us (100%)
    pallas_call x1, Pallas kernels, body(): pl.pallas_call(exchange_kernel, out_shape=(jax.ShapeDtypeStruct((6, 4, 2...  35.2 us
    pallas_call x1, Pallas kernels, body(): pl.pallas_call(decode_kernel, out_shape=jax.ShapeDtypeStruct((4, 2, 2 * t...  6.88 us

profile of v9, /device:TPU:33, one launch (start us, length us, event | category | flops | bytes accessed | tf_op | source)
XLA Modules:
  0.0 42.2 jit_solution(1323510142000574037)
XLA Ops:
  0.0 35.2 %exchange.1 = (f32[6,4,6,64,128]{4,3,2,1,0:T(8,128)S(1)}, f32[3,384]{1,0:T(4,128)S(1)}, bf16[16,1280,256]{2,1,0:T(8,128)(2,1)S(1)}, bf16[16,1536,256]{2,1,0:T(8,128)(2,1)S(1)}) custom-call(bf16[8,32,64]{2,1,0:T(8,128)(2,1)} %tok_hbm.1, bf16[3,3,48,384]{3,2,1,0:T(8,128)(2,1)} %bitcast.1, f32[384]{0:T(512)} %b_hbm.1, f32[384]{0:T(512)} %gain_hbm.1, ...), custom_call_target="tpu_custom_call" | custom-call | tf_op jit(solution)/shard_map/exchange/pallas_call | solution.py:730
  35.2 6.9 %decode.1 = bf16[4,2,128,384]{3,2,1,0:T(8,128)(2,1)} custom-call(f32[6,4,6,64,128]{4,3,2,1,0:T(8,128)S(1)} %get-tuple-element.9.h_ref, f32[3,384]{1,0:T(4,128)S(1)} %get-tuple-element.10.stat_ref, bf16[16,1280,256]{2,1,0:T(8,128)(2,1)S(1)} %get-tuple-element.11.main_ref, bf16[16,1536,256]{2,1,0:T(8,128)(2,1)S(1)} %get-tuple-element.12.rest_ref), custom_call_target="tpu_custom_call" | custom-call | tf_op jit(solution)/shard_map/decode/pallas_call | solution.py:777

commit v10 on v9

--- a/solution.py
+++ b/solution.py
@@ -240,10 +240,16 @@
         for d in range(1, 1 + EARLY):
             tell(know_all, near(0, d, False))
 
+    def tell_across(where):
+        @pl.when(where)
+        def _():
+            tell(know_x, near(1, 0, False))
+            tell(know_x, near(RING_X - 1, 0, False))
+
+    tell_across(z <= 1)
     send_tokens(True)
 
-    tell(know_x, near(1, 0, False))
-    tell(know_x, near(RING_X - 1, 0, False))
+    tell_across(z > 1)
 
     def pass_first(where, onwards):
         @pl.when(where)

time: 42.3 us -> 42.3 us (level)
  no operation moved by 1% of the time
where the time goes in v10:
time: 42.3 us; the launch traced here: 42.2 us
  Pallas kernels  42.1 us (100%)
    pallas_call x1, Pallas kernels, body(): pl.pallas_call(exchange_kernel, out_shape=(jax.ShapeDtypeStruct((6, 4, 2...  35.2 us
    pallas_call x1, Pallas kernels, body(): pl.pallas_call(decode_kernel, out_shape=jax.ShapeDtypeStruct((4, 2, 2 * t...  6.88 us

profile of v10, /device:TPU:33, one launch (start us, length us, event | category | flops | bytes accessed | tf_op | source)
XLA Modules:
  0.0 42.2 jit_solution(13094056488102786960)
XLA Ops:
  0.0 35.2 %exchange.1 = (f32[6,4,6,64,128]{4,3,2,1,0:T(8,128)S(1)}, f32[3,384]{1,0:T(4,128)S(1)}, bf16[16,1280,256]{2,1,0:T(8,128)(2,1)S(1)}, bf16[16,1536,256]{2,1,0:T(8,128)(2,1)S(1)}) custom-call(bf16[8,32,64]{2,1,0:T(8,128)(2,1)} %tok_hbm.1, bf16[3,3,48,384]{3,2,1,0:T(8,128)(2,1)} %bitcast.1, f32[384]{0:T(512)} %b_hbm.1, f32[384]{0:T(512)} %gain_hbm.1, ...), custom_call_target="tpu_custom_call" | custom-call | tf_op jit(solution)/shard_map/exchange/pallas_call | solution.py:736
  35.2 6.9 %decode.1 = bf16[4,2,128,384]{3,2,1,0:T(8,128)(2,1)} custom-call(f32[6,4,6,64,128]{4,3,2,1,0:T(8,128)S(1)} %get-tuple-element.9.h_ref, f32[3,384]{1,0:T(4,128)S(1)} %get-tuple-element.10.stat_ref, bf16[16,1280,256]{2,1,0:T(8,128)(2,1)S(1)} %get-tuple-element.11.main_ref, bf16[16,1536,256]{2,1,0:T(8,128)(2,1)S(1)} %get-tuple-element.12.rest_ref), custom_call_target="tpu_custom_call" | custom-call | tf_op jit(solution)/shard_map/decode/pallas_call | solution.py:783
